TPU v7x, 512 devices: a whole 4x4x16 slice. The times are simulated.
512 devices in a mesh: row: 4 (over y), col: 16 (over z), trial: 8 (over x, core).
Axes of the slice: x: 4, y: 4, z: 16, core: 2. Of those that a mesh axis runs over, the one named last changes fastest.
Arguments:
- pair_rows: bfloat16 [3072, 384, 128], P(('trial', 'row'), 'col'), parts along dimension 0, may hold values from -6 to 6
- left_weight: bfloat16 [1024, 128], P('trial'), parts along dimension 0, may hold values from -0.5 to 0.5
- right_weight: bfloat16 [1024, 128], P('trial'), parts along dimension 0, may hold values from -0.5 to 0.5
- left_gate: bfloat16 [1024, 128], P('trial'), parts along dimension 0, may hold values from -0.5 to 0.5
- right_gate: bfloat16 [1024, 128], P('trial'), parts along dimension 0, may hold values from -0.5 to 0.5
- mid_gain: float32 [128], replicated, may hold values from 0.25 to 1.75
- out_weight: bfloat16 [1024, 128], P('trial'), parts along dimension 0, may hold values from -0.5 to 0.5
- out_gate: bfloat16 [1024, 128], P('trial'), parts along dimension 0, may hold values from -0.5 to 0.5
Outputs:
- pair_change: bfloat16 [3072, 384, 128], P(('trial', 'row'), 'col'), parts along dimension 0
There are 8 independent parts, one for each index of `trial`. A program takes and returns all parts, laid end to end along the dimension named above; an argument that names none is the same for every part. Nothing has to cross between parts.
All inputs are finite; a program needn't handle non-finite values.
Results may differ from a plain program's by a relative error of at most 0.015.
Values may be sent and summed in bfloat16 or wider, within the bound.
A program may use at most 64 MiB of HBM per device.

v0:
```python
import jax
import jax.numpy as jnp
from jax import lax
from jax.sharding import PartitionSpec as P


def norm_channels(values, channel_gain):
    centred = values - jnp.mean(values, axis=-1, keepdims=True)
    return (
        centred
        * lax.rsqrt(jnp.mean(centred * centred, axis=-1, keepdims=True) + 1e-05)
        * channel_gain
    )


def both_factors(pair_in, left_weight, right_weight, left_gate, right_gate):
    left = jnp.einsum("ijc,cd->ijd", pair_in, left_weight, preferred_element_type=jnp.float32)
    left = left * jax.nn.sigmoid(
        jnp.einsum("ijc,cd->ijd", pair_in, left_gate, preferred_element_type=jnp.float32)
    )
    right = jnp.einsum("ijc,cd->ijd", pair_in, right_weight, preferred_element_type=jnp.float32)
    right = right * jax.nn.sigmoid(
        jnp.einsum("ijc,cd->ijd", pair_in, right_gate, preferred_element_type=jnp.float32)
    )
    return (pair_in, left.astype(jnp.bfloat16), right.astype(jnp.bfloat16))


def close_update(mixed, ready, mid_gain, out_weight, out_gate):
    scaled = norm_channels(mixed.astype(jnp.float32), mid_gain).astype(jnp.bfloat16)
    scaled = lax.optimization_barrier(scaled)
    gate = jax.nn.sigmoid(
        jnp.einsum("ijc,cd->ijd", ready, out_gate, preferred_element_type=jnp.float32)
    )
    return (
        jnp.einsum("ijd,dc->ijc", scaled, out_weight, preferred_element_type=jnp.float32) * gate
    ).astype(jnp.bfloat16)


def per_device(
    pair_rows, left_weight, right_weight, left_gate, right_gate, mid_gain, out_weight, out_gate
):
    ready, left, right = both_factors(pair_rows, left_weight, right_weight, left_gate, right_gate)
    count = pair_rows.shape[0] * lax.axis_size("row")
    left_lines, right_lines = (
        lax.all_to_all(left, "row", split_axis=2, concat_axis=0, tiled=True),
        lax.all_to_all(right, "row", split_axis=2, concat_axis=0, tiled=True),
    )
    strip = jnp.einsum(
        "kid,kjd->ijd",
        lax.all_gather(left_lines, "col", axis=1, tiled=True),
        right_lines,
        preferred_element_type=jnp.float32,
    )
    strip = (strip * count ** (-0.5)).astype(jnp.bfloat16)
    mixed = lax.all_to_all(strip, "row", split_axis=0, concat_axis=2, tiled=True)
    return close_update(mixed, ready, mid_gain, out_weight, out_gate)


def solution(mesh):
    placed = (
        P(("trial", "row"), "col", None),
        P("trial", None),
        P("trial", None),
        P("trial", None),
        P("trial", None),
        P(),
        P("trial", None),
        P("trial", None),
    )
    return jax.shard_map(
        per_device,
        mesh=mesh,
        in_specs=placed,
        out_specs=P(("trial", "row"), "col", None),
        check_vma=False,
    )
```

profile of v0, /device:TPU:6, one launch (start us, length us, event | category | flops | bytes accessed | tf_op | source)
XLA Modules:
  0.0 190.1 jit_solution(8397383767578055631)
XLA Ops:
  6.5 1.1 copy-done
  7.6 1.2 fusion.10
  8.8 0.5 fusion.15
  9.3 0.6 copy.31
  9.9 16.6 %all_to_all.45 = bf16[96,24,128]{0,1,2:T(8,128)(2,1)S(1)} all-to-all(bf16[96,24,128]{0,1,2:T(8,128)(2,1)S(1)} %copy.31), channel_id=1, replica_groups=mesh['row'=4,'col'=16,'trial'=8] {'row'}, dimensions={2} | all-to-all | bytes 1179648 | tf_op jit(solution)/shard_map/all_to_all | solution.py:45
  26.4 0.6 copy.33
  27.1 1.3 all_to_all.40
  28.5 0.5 fusion.13
  29.2 0.5 fusion.14
  29.7 0.6 copy.28
  30.3 13.8 %all_to_all.46 = bf16[96,24,128]{0,1,2:T(8,128)(2,1)S(1)} all-to-all(bf16[96,24,128]{0,1,2:T(8,128)(2,1)S(1)} %copy.28), channel_id=1, replica_groups=mesh['row'=4,'col'=16,'trial'=8] {'row'}, dimensions={2} | all-to-all | bytes 1179648 | tf_op jit(solution)/shard_map/all_to_all | solution.py:46
  44.1 0.6 copy.30
  44.7 0.5 all_to_all.36
  45.2 102.1 %all-gather.2.cloned.1.call-done = bf16[384,384,32]{0,1,2:T(8,128)(2,1)} async-done(((bf16[384,24,32]{0,1,2:T(8,128)(2,1)}), bf16[384,384,32]{0,1,2:T(8,128)(2,1)}) %all-gather.2.cloned.1.call-update) | async-done | bytes 9437200 | tf_op jit(solution)/shard_map/all_gather | solution.py:50
  147.4 7.1 %fusion.18 = bf16[384,24,32]{0,1,2:T(8,128)(2,1)S(1)} fusion(bf16[384,24,32]{0,1,2:T(8,128)(2,1)S(1)} %all_to_all.36, bf16[384,384,32]{0,1,2:T(8,128)(2,1)} %all-gather.2.cloned.1.call-done), kind=kOutput, calls=%fused_computation.28 | convolution fusion | flops 227082240 | bytes 10616832 | tf_op jit(solution)/shard_map/kid,kjd->ijd/dot_general | solution.py:48
  154.4 1.5 copy.34
  156.0 3.1 %reshape.28 = bf16[4,2,36864]{2,1,0:T(2,128)(2,1)} reshape(bf16[384,24,32]{2,1,0:T(8,128)(2,1)S(1)} %copy.34) | data formatting | bytes 1179648
  159.1 4.4 %all-to-all-start.2 = ((bf16[4,2,36864]{2,1,0:T(2,128)(2,1)}), bf16[4,2,36864]{2,1,0:T(2,128)(2,1)S(1)}, u32[]{:S(2)}, u32[]{:S(2)}) async-start(bf16[4,2,36864]{2,1,0:T(2,128)(2,1)} %reshape.28), calls=%async_computation.2 | async-start | bytes 1179648 | tf_op jit(solution)/shard_map/all_to_all | solution.py:55
  163.5 1.5 fusion.7
  165.0 8.5 %all-to-all-done.2 = bf16[4,2,36864]{2,1,0:T(2,128)(2,1)S(1)} async-done(((bf16[4,2,36864]{2,1,0:T(2,128)(2,1)}), bf16[4,2,36864]{2,1,0:T(2,128)(2,1)S(1)}, u32[]{:S(2)}, u32[]{:S(2)}) %all-to-all-start.2) | async-done | bytes 589856 | tf_op jit(solution)/shard_map/all_to_all | solution.py:55
  173.5 2.5 %reshape.29 = bf16[384,24,32]{2,1,0:T(8,128)(2,1)} reshape(bf16[4,2,36864]{2,1,0:T(2,128)(2,1)S(1)} %all-to-all-done.2) | data formatting | bytes 1179648
  176.0 2.7 %copy.35 = f32[4,96,24,32]{1,3,0,2:T(8,128)S(1)} copy(bf16[4,96,24,32]{3,2,1,0:T(8,128)(2,1)} %bitcast.56) | data formatting | bytes 1769472 | tf_op jit(solution)/shard_map/convert_element_type | solution.py:29
  180.4 0.4 copy-done.3
  180.7 2.5 %fusion.16 = bf16[96,24,128]{2,1,0:T(8,128)(2,1)} fusion(f32[96,24,128]{2,1,0:T(8,128)} %fusion.7, bf16[96,24,128]{2,1,0:T(8,128)(2,1)S(1)} %copy.36, bf16[128,128]{1,0:T(8,128)(2,1)S(1)} %copy-done.3), kind=kOutput, calls=%fused_computation.26 | convolution fusion | flops 76087296 | bytes 2392064 | tf_op jit(solution)/shard_map/ijd,dc->ijc/dot_general | solution.py:35
  (20 shorter events, 1.9 us)
Async XLA Ops:
  6.5 1.1 copy-start
  6.5 2.3 %copy-start.1 = (bf16[128,128]{1,0:T(8,128)(2,1)S(1)}, bf16[128,128]{1,0:T(8,128)(2,1)}, u32[]{:S(2)}) copy-start(bf16[128,128]{1,0:T(8,128)(2,1)} %param.9) | copy-start | bytes 98308
  6.5 140.8 %all-gather.2.cloned.1.call-start = ((), (), s32[]{:S(2)}) async-start(), calls=%async_computation.3 | async-start | bytes 10027008 | tf_op jit(solution)/shard_map/all_gather | solution.py:50
  27.1 1.4 copy-start.5
  28.4 0.8 copy-start.2
  159.1 4.4 %copy-start.6 = (bf16[128,128]{1,0:T(8,128)(2,1)S(1)}, bf16[128,128]{1,0:T(8,128)(2,1)}, u32[]{:S(2)}) copy-start(bf16[128,128]{1,0:T(8,128)(2,1)} %param.15) | copy-start | bytes 98308
  159.1 14.4 %all-to-all-start.2 = ((bf16[4,2,36864]{2,1,0:T(2,128)(2,1)}), bf16[4,2,36864]{2,1,0:T(2,128)(2,1)S(1)}, u32[]{:S(2)}, u32[]{:S(2)}) async-start(bf16[4,2,36864]{2,1,0:T(2,128)(2,1)} %reshape.28), calls=%async_computation.2 | async-start | bytes 1179648 | tf_op jit(solution)/shard_map/all_to_all | solution.py:55
  179.0 0.7 copy-start.4
  180.0 0.8 copy-start.3
Sparse Core Ops, SparseCore 0:
  28.6 118.7 all-gather.1
where the time goes:
time: 191 us; the launch traced here: 190 us
  waiting for transfers between devices  111 us (58%)
  blocking collectives  30.4 us (16%)
  local copies, waits for them, and re-layouts  16.6 us (9%)
  matrix products  13.7 us (7%)
  between operations  13.6 us (7%)
  starting transfers between devices  4.42 us (2%)
    all_gather x1, waiting for transfers between devices, per_device(): lax.all_gather(left_lines, 'col', axis=1, tiled=True)  102 us
    all_to_all x1, blocking collectives, per_device(): lax.all_to_all(left, 'row', split_axis=2, concat_axis=0, tiled=True)  16.6 us
    all_to_all x1, blocking collectives, per_device(): lax.all_to_all(right, 'row', split_axis=2, concat_axis=0, tiled=True)  13.8 us
    all_to_all x1, waiting for transfers between devices, per_device(): lax.all_to_all(strip, 'row', split_axis=0, concat_axis=2, tiled=True)  8.52 us
    unnamed x16, local copies, waits for them, and re-layouts  7.75 us
    dot_general x1, matrix products, per_device(): jnp.einsum('kid,kjd->ijd', lax.all_gather(left_lines, 'col', axis=1, tile...  7.05 us
    all_to_all x1, starting transfers between devices, per_device(): lax.all_to_all(strip, 'row', split_axis=0, concat_axis=2, tiled=True)  4.41 us
  transfers between devices with their start and end apart: 2, of which 2 were waited for; matrix products, arithmetic and copies ran while one was open for 2% of the time, Pallas kernels for 0%

commit v1 on v0

v1 whole, which is shorter than its diff:
```python
import functools

import jax
import jax.numpy as jnp
from jax import lax
from jax.experimental import pallas as pl
from jax.experimental.pallas import tpu as pltpu
from jax.sharding import PartitionSpec as P

MESH = pl.DeviceIdType.MESH
F32, BF16 = jnp.float32, jnp.bfloat16
ROWS, COLS = 4, 16
LINES, WIDE, CH = 96, 24, 128
FAR = 7
CHUNK = 2 * WIDE
SUBS = ((0, 4), (4, 8), (8, 12), (12, 16))


def sigmoid(x):
    return 0.5 + 0.5 * jnp.tanh(0.5 * x)


def nt(a, b):
    return lax.dot_general(a, b, (((1,), (1,)), ((), ())), preferred_element_type=F32)


def kernel(
    x_ref, lw_ref, lg_ref, rw_ref, rg_ref, gain_ref, ow_ref, og_ref,
    o_ref,
    xf, wt, gb, fac, zs, yb, zb, lb, rb, lm, rm, cs, cb, es, ds, gt, stat,
    ysend, yrecv, zsend, zrecv, xsend, xrecv, csend, crecv, esend, erecv,
):
    y = lax.axis_index("row")
    z = lax.axis_index("col")

    def row_at(o):
        return lax.rem(y + o, ROWS)

    def col_at(s):
        return lax.rem(z + s + COLS, COLS)

    steps = [(s, way) for s in range(FAR, 0, -1) for way in (0, 1)]

    barrier = pltpu.get_barrier_semaphore()
    for o in range(1, ROWS):
        pl.semaphore_signal(barrier, inc=1, device_id={"row": row_at(o)}, device_id_type=MESH)
    for s, way in steps:
        pl.semaphore_signal(
            barrier, inc=1, device_id={"col": col_at(s if way == 0 else -s)}, device_id_type=MESH
        )

    def arc_of(t):
        s = FAR - t // 2
        way = t % 2
        return lax.rem(z + COLS + (1 - 2 * way) * s - way, COLS)

    xf[pl.ds(0, LINES * WIDE), :] = x_ref[...].astype(F32)
    xf[pl.ds(LINES * WIDE, 32 * WIDE), :] = jnp.zeros((32 * WIDE, CH), F32)
    for n, ref in enumerate((lw_ref, lg_ref, rw_ref, rg_ref)):
        wt[pl.ds(CH * n, CH), :] = ref[...].astype(F32).T.astype(BF16)
    gb[...] = jnp.broadcast_to(gain_ref[...], (CH, CH)).T

    def project(arr):
        @pl.loop(0, WIDE)
        def _(i):
            parts = []
            for b in range(4):
                block = lax.rem(b + y, 4)
                parts.append(xf[pl.ds(block * (32 * WIDE) + i, 32, stride=WIDE), :])
            xi = jnp.concatenate(parts, axis=0).astype(BF16)
            both = nt(wt[pl.ds(2 * CH * arr, 2 * CH), :], xi)
            fac[arr, pl.ds(i, CH, stride=WIDE), :] = both[:CH] * sigmoid(both[CH:])

    def y_copy(arr, sub, o):
        t0, t1 = SUBS[sub]
        dest = row_at(o)
        return pltpu.make_async_remote_copy(
            src_ref=zs.at[arr, dest, pl.ds(t0, t1 - t0)],
            dst_ref=yb.at[arr, y, pl.ds(t0, t1 - t0)],
            send_sem=ysend.at[arr, sub, o - 1],
            recv_sem=yrecv.at[arr, sub, o - 1],
            device_id={"row": dest},
            device_id_type=MESH,
        )

    def split_rows(arr, sub):
        t0, t1 = SUBS[sub]

        @pl.loop(t0, t1)
        def _(t):
            arc = arc_of(t)
            for q in range(ROWS):
                first = pl.multiple_of((32 * q + 2 * arc) * WIDE, 16)
                zs[arr, q, t] = fac[arr, pl.ds(first, CHUNK), :].astype(BF16)
            first = pl.multiple_of((32 * y + 2 * arc) * WIDE, 16)
            yb[arr, y, t] = fac[arr, pl.ds(first, CHUNK), :].astype(BF16)

    project(0)
    split_rows(0, 0)
    pl.semaphore_wait(barrier, ROWS - 1 + len(steps))
    for sub in range(len(SUBS)):
        if sub:
            split_rows(0, sub)
        for o in range(1, ROWS):
            y_copy(0, sub, o).start()
    project(1)
    for sub in range(len(SUBS)):
        split_rows(1, sub)
        for o in range(1, ROWS):
            y_copy(1, sub, o).start()

    def z_copy(arr, s, way):
        t = 2 * (FAR - s) + way
        dst = lb.at[way, z] if arr == 0 else rb.at[way, s]
        return pltpu.make_async_remote_copy(
            src_ref=zb.at[arr, t],
            dst_ref=dst,
            send_sem=zsend.at[arr, t],
            recv_sem=zrecv.at[arr, t],
            device_id={"col": col_at(s if way == 0 else -s)},
            device_id_type=MESH,
        )

    lane = lax.broadcasted_iota(jnp.int32, (CHUNK, CH), 1)

    def join(arr, t):
        a, b, c, d = (yb[arr, q, t].astype(F32) for q in range(ROWS))
        return jnp.concatenate(
            [
                jnp.where(lane < 96, a, b),
                jnp.where(lane < 64, b, c),
                jnp.where(lane < 32, c, d),
            ],
            axis=1,
        ).astype(BF16)

    for arr in (0, 1):
        for sub, (t0, t1) in enumerate(SUBS):
            for o in range(1, ROWS):
                y_copy(arr, sub, o).wait_recv()

            @pl.loop(t0, min(t1, 2 * FAR))
            def _(t):
                zb[arr, t] = join(arr, t)

            for t in range(max(t0, 2 * FAR), t1):
                way = t % 2
                if arr == 0:
                    lb[way, z] = join(arr, t)
                else:
                    rb[way, 0] = join(arr, t)
            for t in range(t0, min(t1, 2 * FAR)):
                z_copy(arr, FAR - t // 2, t % 2).start()

    @pl.loop(0, 6)
    def _(n):
        rows = pl.ds(pl.multiple_of(n * 384, 384), 384)
        g = jnp.dot(x_ref[rows, :], og_ref[...], preferred_element_type=F32)
        gt[rows, :] = sigmoid(g)

    def x_copy(s, way):
        src = col_at(-s if way == 0 else s)
        return pltpu.make_async_remote_copy(
            src_ref=lb.at[way, src],
            dst_ref=lb.at[1 - way, src],
            send_sem=xsend.at[way, s],
            recv_sem=xrecv.at[way, s],
            device_id={"col": col_at(1 if way == 0 else -1)},
            device_id_type=MESH,
        )

    for way in (0, 1):
        x_copy(0, way).start()
    for s, way in steps[::-1]:
        z_copy(0, s, way).wait_recv()
        x_copy(s, way).start()

    for s, way in steps[::-1]:
        z_copy(1, s, way).wait_recv()

    @pl.loop(0, 2)
    def _(way):
        for s in range(0, 8, 2):
            one, two = rb[way, s].astype(F32), rb[way, s + 1].astype(F32)
            for ph in (0, 1):
                cut = slice(WIDE * ph, WIDE * ph + WIDE)
                rm[way, ph, pl.ds(WIDE * s, CHUNK), :] = jnp.concatenate(
                    [one[cut], two[cut]], axis=0
                ).astype(BF16)

    for way in (0, 1):
        for s in range(8):
            x_copy(s, way).wait_recv()

    def c_copy(s, way):
        t = 2 * (FAR - s) + way
        return pltpu.make_async_remote_copy(
            src_ref=cs.at[t],
            dst_ref=cb.at[t],
            send_sem=csend.at[t],
            recv_sem=crecv.at[t],
            device_id={"col": col_at(-s if way == 0 else s)},
            device_id_type=MESH,
        )

    scale = (ROWS * LINES) ** -0.5
    for way in (0, 1):
        for q in range(ROWS):
            four = [lb[way, 4 * q + n].astype(F32) for n in range(4)]
            for ph in (0, 1):
                cut = slice(WIDE * ph, WIDE * ph + WIDE)
                lines = jnp.concatenate([f[cut] for f in four], axis=0).astype(BF16)
                for u in range(3):
                    lm[way, ph, pl.ds(128 * u + 32 * ((q + u) % 4), 32), :] = lines[
                        32 * u : 32 * u + 32
                    ]
        sums = [nt(rm[way, ph], lm[way, ph]) * scale for ph in (0, 1)]
        for s in range(FAR, -1, -1):
            cut = slice(WIDE * s, WIDE * s + WIDE)
            chunk = jnp.concatenate([sums[0][cut], sums[1][cut]], axis=0).astype(BF16)
            if s == 0:
                cb[2 * FAR + way] = chunk
            else:
                cs[2 * (FAR - s) + way] = chunk
        for s in range(FAR, 0, -1):
            c_copy(s, way).start()

    def e_copy(sub, o):
        t0, t1 = SUBS[sub]
        dest = row_at(o)
        return pltpu.make_async_remote_copy(
            src_ref=es.at[dest, pl.ds(t0, t1 - t0)],
            dst_ref=ds.at[y, pl.ds(t0, t1 - t0)],
            send_sem=esend.at[sub, o - 1],
            recv_sem=erecv.at[sub, o - 1],
            device_id={"row": dest},
            device_id_type=MESH,
        )

    strip = lane // 32

    for sub, (t0, t1) in enumerate(SUBS):
        for t in range(t0, min(t1, 2 * FAR)):
            c_copy(FAR - t // 2, t % 2).wait_recv()

        @pl.loop(t0, t1)
        def _(t):
            a, b, c = (cb[t, :, pl.ds(128 * u, 128)].astype(F32) for u in range(3))

            def quarter(q):
                return jnp.where(
                    strip == q, a, jnp.where(strip == lax.rem(q + 1, 4), b, c)
                ).astype(BF16)

            for q in range(ROWS):
                es[q, t] = quarter(q)
            ds[y, t] = quarter(y)

        for o in range(1, ROWS):
            e_copy(sub, o).start()

    mixed = fac.at[0]
    total = jnp.zeros((WIDE, CH), F32)
    for sub, (t0, t1) in enumerate(SUBS):
        for o in range(1, ROWS):
            e_copy(sub, o).wait_recv()

        def add(t, total):
            arc = arc_of(t)
            for q in range(ROWS):
                block = ds[q, t].astype(F32)
                first = pl.multiple_of((32 * q + 2 * arc) * WIDE, 16)
                mixed[pl.ds(first, CHUNK), :] = block
                total = total + block[:WIDE] + block[WIDE:]
            return total

        total = lax.fori_loop(t0, t1, add, total)
    mean = total * (1.0 / CH)

    def spread(n, total):
        for m in range(8):
            off = mixed[pl.ds(pl.multiple_of((8 * n + m) * WIDE, 8), WIDE), :] - mean
            total = total + off * off
        return total

    var = lax.fori_loop(0, CH // 8, spread, jnp.zeros((WIDE, CH), F32)) * (1.0 / CH)
    stat[0] = mean
    stat[1] = lax.rsqrt(var + 1e-05)

    out = fac.at[1]

    @pl.loop(0, WIDE)
    def _(j):
        block = mixed[pl.ds(j, CH, stride=WIDE), :]
        block = (block - stat[0, pl.ds(j, 1), :]) * stat[1, pl.ds(j, 1), :] * gb[...]
        change = jnp.dot(block.T.astype(BF16), ow_ref[...], preferred_element_type=F32)
        for b in range(4):
            u = lax.rem(b - y + 4, 4)
            out[pl.ds(u * (32 * WIDE) + j, 32, stride=WIDE), :] = change[32 * b : 32 * b + 32]

    @pl.loop(0, 6)
    def _(n):
        rows = pl.ds(pl.multiple_of(n * 384, 384), 384)
        o_ref[rows, :] = (out[rows, :] * gt[rows, :]).astype(BF16)

    for arr in (0, 1):
        for sub in range(len(SUBS)):
            for o in range(1, ROWS):
                y_copy(arr, sub, o).wait_send()
        for s, way in steps:
            z_copy(arr, s, way).wait_send()
    for way in (0, 1):
        for s in range(8):
            x_copy(s, way).wait_send()
    for s, way in steps:
        c_copy(s, way).wait_send()
    for sub in range(len(SUBS)):
        for o in range(1, ROWS):
            e_copy(sub, o).wait_send()


def per_device(
    pair_rows, left_weight, right_weight, left_gate, right_gate, mid_gain, out_weight, out_gate
):
    pixels = pair_rows.shape[0] * pair_rows.shape[1]
    dma = pltpu.SemaphoreType.DMA
    subs = len(SUBS)
    out = pl.pallas_call(
        kernel,
        out_shape=jax.ShapeDtypeStruct((pixels, CH), BF16),
        in_specs=[pl.BlockSpec(memory_space=pltpu.VMEM)] * 8,
        out_specs=pl.BlockSpec(memory_space=pltpu.VMEM),
        scratch_shapes=[
            pltpu.VMEM((128 * WIDE, CH), F32),
            pltpu.VMEM((4 * CH, CH), BF16),
            pltpu.VMEM((CH, CH), F32),
            pltpu.VMEM((2, CH * WIDE, CH), F32),
            pltpu.VMEM((2, ROWS, COLS, CHUNK, CH), BF16),
            pltpu.VMEM((2, ROWS, COLS, CHUNK, CH), BF16),
            pltpu.VMEM((2, COLS, CHUNK, 384), BF16),
            pltpu.VMEM((2, COLS, CHUNK, 384), BF16),
            pltpu.VMEM((2, 8, CHUNK, 384), BF16),
            pltpu.VMEM((2, 2, 384, 384), BF16),
            pltpu.VMEM((2, 2, 192, 384), BF16),
            pltpu.VMEM((COLS, CHUNK, 384), BF16),
            pltpu.VMEM((COLS, CHUNK, 384), BF16),
            pltpu.VMEM((ROWS, COLS, CHUNK, CH), BF16),
            pltpu.VMEM((ROWS, COLS, CHUNK, CH), BF16),
            pltpu.VMEM((pixels, CH), F32),
            pltpu.VMEM((2, WIDE, CH), F32),
            dma((2, subs, 3)), dma((2, subs, 3)),
            dma((2, 14)), dma((2, 14)),
            dma((2, 8)), dma((2, 8)),
            dma((14,)), dma((14,)),
            dma((subs, 3)), dma((subs, 3)),
        ],
        compiler_params=pltpu.CompilerParams(
            collective_id=0, has_side_effects=True, vmem_limit_bytes=48 * 1024 * 1024
        ),
    )(
        pair_rows.reshape(pixels, CH),
        left_weight, left_gate, right_weight, right_gate,
        mid_gain.reshape(1, CH), out_weight, out_gate,
    )
    return out.reshape(pair_rows.shape)


def solution(mesh):
    placed = (
        P(("trial", "row"), "col", None),
        P("trial", None),
        P("trial", None),
        P("trial", None),
        P("trial", None),
        P(),
        P("trial", None),
        P("trial", None),
    )
    return jax.shard_map(
        per_device,
        mesh=mesh,
        in_specs=placed,
        out_specs=P(("trial", "row"), "col", None),
        check_vma=False,
    )
```

time: 191 us -> 120 us (0.63)
  Pallas kernels: 0 us -> 112 us
  waiting for transfers between devices: 111 us -> 0 us
  blocking collectives: 30.4 us -> 0 us
  matrix products: 13.7 us -> 0 us
  between operations: 13.6 us -> 0.02 us
  local copies, waits for them, and re-layouts: 16.6 us -> 7.08 us
  starting transfers between devices: 4.42 us -> 0 us
    pallas_call x0 -> x1, Pallas kernels: none -> 112 us  [per_device(): pl.pallas_call(kernel, out_shape=jax.ShapeDtypeStruct((pixels, CH), BF16)...]
    all_gather x1 -> x0, waiting for transfers between devices: 102 us -> none  [per_device(): lax.all_gather(left_lines, 'col', axis=1, tiled=True)]
    all_to_all x2 -> x0, blocking collectives: 30.4 us -> none  [the longest x1 16.6 us: per_device(): lax.all_to_all(left, 'row', split_axis=2, concat_axis=0, tiled=True)]
    dot_general x7 -> x0, matrix products: 13.7 us -> none  [the longest x1 7.05 us: per_device(): jnp.einsum('kid,kjd->ijd', lax.all_gather(left_lines, 'col', axis=1, tile...]
    all_to_all x1 -> x0, waiting for transfers between devices: 8.52 us -> none  [per_device(): lax.all_to_all(strip, 'row', split_axis=0, concat_axis=2, tiled=True)]
    convert_element_type x4 -> x0, local copies, waits for them, and re-layouts: 5.44 us -> none  [the longest x1 2.72 us: close_update(): mixed.astype(jnp.float32)]
    all_to_all x1 -> x0, starting transfers between devices: 4.41 us -> none  [per_device(): lax.all_to_all(strip, 'row', split_axis=0, concat_axis=2, tiled=True)]
    all_to_all x4 -> x0, local copies, waits for them, and re-layouts: 3.07 us -> none  [the longest x2 1.95 us: per_device(): lax.all_to_all(left, 'row', split_axis=2, concat_axis=0, tiled=True)]
  transfers between devices with their start and end apart: 2 -> 0, of which waited for: 2 -> 0; matrix products, arithmetic and copies ran while one was open for 2% -> 0% of each run, Pallas kernels for 0% -> 0%
where the time goes in v1:
time: 120 us; the launch traced here: 119 us
  Pallas kernels  112 us (93%)
  local copies, waits for them, and re-layouts  7.08 us (6%)
    pallas_call x1, Pallas kernels, per_device(): pl.pallas_call(kernel, out_shape=jax.ShapeDtypeStruct((pixels, CH), BF16)...  112 us
    unnamed x17, local copies, waits for them, and re-layouts  7.08 us

profile of v1, /device:TPU:6, one launch (start us, length us, event | category | flops | bytes accessed | tf_op | source)
XLA Modules:
  0.0 119.1 jit_solution(11095354203330349488)
XLA Ops:
  0.0 0.0 copy-start.7
  0.0 0.7 copy-done.7
  0.7 0.0 copy-start
  0.7 1.1 copy-done
  1.7 0.0 copy-start.1
  1.7 0.8 copy-done.1
  2.5 0.0 copy-start.2
  2.5 0.8 copy-done.2
  3.2 0.0 copy-start.3
  3.2 0.8 copy-done.3
  4.0 0.0 copy-start.4
  4.0 0.8 copy-done.4
  4.8 0.0 copy-start.5
  4.8 0.8 copy-done.5
  5.5 0.0 copy-start.6
  5.5 0.8 copy-done.6
  6.3 112.0 %shard_map.82 = bf16[2304,128]{1,0:T(8,128)(2,1)S(1)} custom-call(bf16[2304,128]{1,0:T(8,128)(2,1)S(1)} %bitcast.4, bf16[128,128]{1,0:T(8,128)(2,1)S(1)} %copy-done.1, bf16[128,128]{1,0:T(8,128)(2,1)S(1)} %copy-done.2, bf16[128,128]{1,0:T(8,128)(2,1)S(1)} %copy-done.3, bf16[128,128]{1,0:T(8,128)(2,1)S(1)} %copy-done.4, f32[1,128]{1,0:T(1,128)S(1)} %bitcast.5, ...), custom_call_target="tpu_custom_call" | custom-call | tf_op jit(solution)/shard_map/pallas_call | solution.py:328
  118.3 0.8 copy.10
Async XLA Ops:
  0.0 0.7 copy-start.7
  0.7 1.1 copy-start
  1.7 0.8 copy-start.1
  2.5 0.8 copy-start.2
  3.2 0.8 copy-start.3
  4.0 0.8 copy-start.4
  4.8 0.8 copy-start.5
  5.5 0.8 copy-start.6

commit v2 on v1

--- a/solution.py
+++ b/solution.py
@@ -13,7 +13,8 @@
 LINES, WIDE, CH = 96, 24, 128
 FAR = 7
 CHUNK = 2 * WIDE
-SUBS = ((0, 4), (4, 8), (8, 12), (12, 16))
+YSUBS = (((0, 2), (2, 6), (6, 12), (12, 16)), ((12, 16), (8, 12), (4, 8), (0, 4)))
+ESUBS = ((14, 16), (12, 14), (8, 12), (6, 8), (4, 6), (2, 4), (0, 2))
 
 
 def sigmoid(x):
@@ -25,10 +26,10 @@
 
 
 def kernel(
-    x_ref, lw_ref, lg_ref, rw_ref, rg_ref, gain_ref, ow_ref, og_ref,
+    x_hbm, lw_hbm, lg_hbm, rw_hbm, rg_hbm, gain_hbm, ow_hbm, og_hbm,
     o_ref,
-    xf, wt, gb, fac, zs, yb, zb, lb, rb, lm, rm, cs, cb, es, ds, gt, stat,
-    ysend, yrecv, zsend, zrecv, xsend, xrecv, csend, crecv, esend, erecv,
+    x_ref, wraw, gain_ref, xf, wt, gb, facl, facr, zs, yb, zb, lb, rb, lm, rm, cs, cb, es, ds, gt, stat,
+    insem, ysend, yrecv, zsend, zrecv, xsend, xrecv, csend, crecv, esend, erecv,
 ):
     y = lax.axis_index("row")
     z = lax.axis_index("col")
@@ -40,6 +41,13 @@
         return lax.rem(z + s + COLS, COLS)
 
     steps = [(s, way) for s in range(FAR, 0, -1) for way in (0, 1)]
+
+    mats = (lw_hbm, lg_hbm, rw_hbm, rg_hbm, ow_hbm, og_hbm)
+    loads = [pltpu.make_async_copy(x_hbm, x_ref, insem.at[0])]
+    loads += [pltpu.make_async_copy(gain_hbm, gain_ref, insem.at[1])]
+    loads += [pltpu.make_async_copy(m, wraw.at[n], insem.at[2 + n]) for n, m in enumerate(mats)]
+    for load in loads:
+        load.start()
 
     barrier = pltpu.get_barrier_semaphore()
     for o in range(1, ROWS):
@@ -54,25 +62,32 @@
         way = t % 2
         return lax.rem(z + COLS + (1 - 2 * way) * s - way, COLS)
 
+    facs = (facl, facr)
+
+    xf[pl.ds(LINES * WIDE, 32 * WIDE), :] = jnp.zeros((32 * WIDE, CH), F32)
+    for load in loads:
+        load.wait()
     xf[pl.ds(0, LINES * WIDE), :] = x_ref[...].astype(F32)
-    xf[pl.ds(LINES * WIDE, 32 * WIDE), :] = jnp.zeros((32 * WIDE, CH), F32)
-    for n, ref in enumerate((lw_ref, lg_ref, rw_ref, rg_ref)):
-        wt[pl.ds(CH * n, CH), :] = ref[...].astype(F32).T.astype(BF16)
+    for n in range(4):
+        wt[pl.ds(CH * n, CH), :] = wraw[n].astype(F32).T.astype(BF16)
     gb[...] = jnp.broadcast_to(gain_ref[...], (CH, CH)).T
 
     def project(arr):
-        @pl.loop(0, WIDE)
-        def _(i):
+        @pl.loop(0, WIDE // 2, unroll=3)
+        def _(n):
             parts = []
-            for b in range(4):
-                block = lax.rem(b + y, 4)
-                parts.append(xf[pl.ds(block * (32 * WIDE) + i, 32, stride=WIDE), :])
+            for i in (2 * n, 2 * n + 1):
+                for b in range(4):
+                    block = lax.rem(b + y, 4)
+                    parts.append(xf[pl.ds(block * (32 * WIDE) + i, 32, stride=WIDE), :])
             xi = jnp.concatenate(parts, axis=0).astype(BF16)
             both = nt(wt[pl.ds(2 * CH * arr, 2 * CH), :], xi)
-            fac[arr, pl.ds(i, CH, stride=WIDE), :] = both[:CH] * sigmoid(both[CH:])
+            value = both[:CH] * sigmoid(both[CH:])
+            for m in range(2):
+                facs[arr][pl.ds(2 * n + m, CH, stride=WIDE), :] = value[:, CH * m : CH * m + CH]
 
     def y_copy(arr, sub, o):
-        t0, t1 = SUBS[sub]
+        t0, t1 = YSUBS[arr][sub]
         dest = row_at(o)
         return pltpu.make_async_remote_copy(
             src_ref=zs.at[arr, dest, pl.ds(t0, t1 - t0)],
@@ -84,30 +99,16 @@
         )
 
     def split_rows(arr, sub):
-        t0, t1 = SUBS[sub]
+        t0, t1 = YSUBS[arr][sub]
 
         @pl.loop(t0, t1)
         def _(t):
             arc = arc_of(t)
             for q in range(ROWS):
                 first = pl.multiple_of((32 * q + 2 * arc) * WIDE, 16)
-                zs[arr, q, t] = fac[arr, pl.ds(first, CHUNK), :].astype(BF16)
+                zs[arr, q, t] = facs[arr][pl.ds(first, CHUNK), :].astype(BF16)
             first = pl.multiple_of((32 * y + 2 * arc) * WIDE, 16)
-            yb[arr, y, t] = fac[arr, pl.ds(first, CHUNK), :].astype(BF16)
-
-    project(0)
-    split_rows(0, 0)
-    pl.semaphore_wait(barrier, ROWS - 1 + len(steps))
-    for sub in range(len(SUBS)):
-        if sub:
-            split_rows(0, sub)
-        for o in range(1, ROWS):
-            y_copy(0, sub, o).start()
-    project(1)
-    for sub in range(len(SUBS)):
-        split_rows(1, sub)
-        for o in range(1, ROWS):
-            y_copy(1, sub, o).start()
+            yb[arr, y, t] = facs[arr][pl.ds(first, CHUNK), :].astype(BF16)
 
     def z_copy(arr, s, way):
         t = 2 * (FAR - s) + way
@@ -134,28 +135,48 @@
             axis=1,
         ).astype(BF16)
 
-    for arr in (0, 1):
-        for sub, (t0, t1) in enumerate(SUBS):
-            for o in range(1, ROWS):
-                y_copy(arr, sub, o).wait_recv()
-
-            @pl.loop(t0, min(t1, 2 * FAR))
-            def _(t):
-                zb[arr, t] = join(arr, t)
-
-            for t in range(max(t0, 2 * FAR), t1):
-                way = t % 2
-                if arr == 0:
-                    lb[way, z] = join(arr, t)
-                else:
-                    rb[way, 0] = join(arr, t)
-            for t in range(t0, min(t1, 2 * FAR)):
-                z_copy(arr, FAR - t // 2, t % 2).start()
+    def over_col(arr, sub):
+        t0, t1 = YSUBS[arr][sub]
+        for o in range(1, ROWS):
+            y_copy(arr, sub, o).wait_recv()
+
+        @pl.loop(t0, min(t1, 2 * FAR))
+        def _(t):
+            zb[arr, t] = join(arr, t)
+
+        for t in range(max(t0, 2 * FAR), t1):
+            way = t % 2
+            if arr == 0:
+                lb[way, z] = join(arr, t)
+            else:
+                rb[way, 0] = join(arr, t)
+        sends = list(range(t0, min(t1, 2 * FAR)))
+        for t in sends if arr == 0 else sends[::-1]:
+            z_copy(arr, FAR - t // 2, t % 2).start()
+
+    project(0)
+    split_rows(0, 0)
+    pl.semaphore_wait(barrier, ROWS - 1 + len(steps))
+    for sub in range(4):
+        if sub:
+            split_rows(0, sub)
+        for o in range(1, ROWS):
+            y_copy(0, sub, o).start()
+    project(1)
+    over_col(0, 0)
+    for sub in range(4):
+        split_rows(1, sub)
+        for o in range(1, ROWS):
+            y_copy(1, sub, o).start()
+        if sub < 3:
+            over_col(0, sub + 1)
+    over_col(1, 0)
+    over_col(1, 1)
 
     @pl.loop(0, 6)
     def _(n):
         rows = pl.ds(pl.multiple_of(n * 384, 384), 384)
-        g = jnp.dot(x_ref[rows, :], og_ref[...], preferred_element_type=F32)
+        g = jnp.dot(x_ref[rows, :], wraw[5], preferred_element_type=F32)
         gt[rows, :] = sigmoid(g)
 
     def x_copy(s, way):
@@ -175,22 +196,22 @@
         z_copy(0, s, way).wait_recv()
         x_copy(s, way).start()
 
-    for s, way in steps[::-1]:
-        z_copy(1, s, way).wait_recv()
-
-    @pl.loop(0, 2)
-    def _(way):
-        for s in range(0, 8, 2):
-            one, two = rb[way, s].astype(F32), rb[way, s + 1].astype(F32)
-            for ph in (0, 1):
-                cut = slice(WIDE * ph, WIDE * ph + WIDE)
-                rm[way, ph, pl.ds(WIDE * s, CHUNK), :] = jnp.concatenate(
-                    [one[cut], two[cut]], axis=0
-                ).astype(BF16)
-
-    for way in (0, 1):
-        for s in range(8):
-            x_copy(s, way).wait_recv()
+    over_col(1, 2)
+    over_col(1, 3)
+
+    def near_blocks(half):
+        for s in range(4 * half, 4 * half + 4):
+            if s:
+                for way in (0, 1):
+                    z_copy(1, s, way).wait_recv()
+        for way in (0, 1):
+            for s in range(4 * half, 4 * half + 4, 2):
+                one, two = rb[way, s].astype(F32), rb[way, s + 1].astype(F32)
+                for ph in (0, 1):
+                    cut = slice(WIDE * ph, WIDE * ph + WIDE)
+                    rm[way, ph, pl.ds(WIDE * s, CHUNK), :] = jnp.concatenate(
+                        [one[cut], two[cut]], axis=0
+                    ).astype(BF16)
 
     def c_copy(s, way):
         t = 2 * (FAR - s) + way
@@ -204,7 +225,10 @@
         )
 
     scale = (ROWS * LINES) ** -0.5
+    near_blocks(0)
     for way in (0, 1):
+        for s in range(8):
+            x_copy(s, 1 - way).wait_recv()
         for q in range(ROWS):
             four = [lb[way, 4 * q + n].astype(F32) for n in range(4)]
             for ph in (0, 1):
@@ -214,19 +238,27 @@
                     lm[way, ph, pl.ds(128 * u + 32 * ((q + u) % 4), 32), :] = lines[
                         32 * u : 32 * u + 32
                     ]
-        sums = [nt(rm[way, ph], lm[way, ph]) * scale for ph in (0, 1)]
-        for s in range(FAR, -1, -1):
-            cut = slice(WIDE * s, WIDE * s + WIDE)
-            chunk = jnp.concatenate([sums[0][cut], sums[1][cut]], axis=0).astype(BF16)
-            if s == 0:
-                cb[2 * FAR + way] = chunk
-            else:
-                cs[2 * (FAR - s) + way] = chunk
-        for s in range(FAR, 0, -1):
-            c_copy(s, way).start()
+
+    for half in (0, 1):
+        if half:
+            near_blocks(1)
+        for way in (0, 1):
+            rows = pl.ds(96 * half, 96)
+            sums = [nt(rm[way, ph, rows, :], lm[way, ph]) * scale for ph in (0, 1)]
+            for n in range(4):
+                s = 4 * half + n
+                cut = slice(WIDE * n, WIDE * n + WIDE)
+                chunk = jnp.concatenate([sums[0][cut], sums[1][cut]], axis=0).astype(BF16)
+                if s == 0:
+                    cb[2 * FAR + way] = chunk
+                else:
+                    cs[2 * (FAR - s) + way] = chunk
+        for s in range(max(4 * half, 1), 4 * half + 4):
+            for way in (0, 1):
+                c_copy(s, way).start()
 
     def e_copy(sub, o):
-        t0, t1 = SUBS[sub]
+        t0, t1 = ESUBS[sub]
         dest = row_at(o)
         return pltpu.make_async_remote_copy(
             src_ref=es.at[dest, pl.ds(t0, t1 - t0)],
@@ -239,7 +271,7 @@
 
     strip = lane // 32
 
-    for sub, (t0, t1) in enumerate(SUBS):
+    for sub, (t0, t1) in enumerate(ESUBS):
         for t in range(t0, min(t1, 2 * FAR)):
             c_copy(FAR - t // 2, t % 2).wait_recv()
 
@@ -259,9 +291,9 @@
         for o in range(1, ROWS):
             e_copy(sub, o).start()
 
-    mixed = fac.at[0]
+    mixed = facl
     total = jnp.zeros((WIDE, CH), F32)
-    for sub, (t0, t1) in enumerate(SUBS):
+    for sub, (t0, t1) in enumerate(ESUBS):
         for o in range(1, ROWS):
             e_copy(sub, o).wait_recv()
 
@@ -287,16 +319,22 @@
     stat[0] = mean
     stat[1] = lax.rsqrt(var + 1e-05)
 
-    out = fac.at[1]
-
-    @pl.loop(0, WIDE)
-    def _(j):
-        block = mixed[pl.ds(j, CH, stride=WIDE), :]
-        block = (block - stat[0, pl.ds(j, 1), :]) * stat[1, pl.ds(j, 1), :] * gb[...]
-        change = jnp.dot(block.T.astype(BF16), ow_ref[...], preferred_element_type=F32)
-        for b in range(4):
-            u = lax.rem(b - y + 4, 4)
-            out[pl.ds(u * (32 * WIDE) + j, 32, stride=WIDE), :] = change[32 * b : 32 * b + 32]
+    out = facr
+
+    @pl.loop(0, WIDE // 4)
+    def _(n):
+        scaled = []
+        for j in range(4):
+            block = mixed[pl.ds(4 * n + j, CH, stride=WIDE), :]
+            block = (block - stat[0, pl.ds(4 * n + j, 1), :]) * stat[1, pl.ds(4 * n + j, 1), :] * gb[...]
+            scaled.append(block.astype(BF16).T)
+        change = jnp.dot(jnp.concatenate(scaled, axis=0), wraw[4], preferred_element_type=F32)
+        for j in range(4):
+            for b in range(4):
+                u = lax.rem(b - y + 4, 4)
+                out[pl.ds(u * (32 * WIDE) + 4 * n + j, 32, stride=WIDE), :] = change[
+                    CH * j + 32 * b : CH * j + 32 * b + 32
+                ]
 
     @pl.loop(0, 6)
     def _(n):
@@ -304,7 +342,7 @@
         o_ref[rows, :] = (out[rows, :] * gt[rows, :]).astype(BF16)
 
     for arr in (0, 1):
-        for sub in range(len(SUBS)):
+        for sub in range(4):
             for o in range(1, ROWS):
                 y_copy(arr, sub, o).wait_send()
         for s, way in steps:
@@ -314,7 +352,7 @@
             x_copy(s, way).wait_send()
     for s, way in steps:
         c_copy(s, way).wait_send()
-    for sub in range(len(SUBS)):
+    for sub in range(len(ESUBS)):
         for o in range(1, ROWS):
             e_copy(sub, o).wait_send()
 
@@ -324,17 +362,21 @@
 ):
     pixels = pair_rows.shape[0] * pair_rows.shape[1]
     dma = pltpu.SemaphoreType.DMA
-    subs = len(SUBS)
+    subs = len(ESUBS)
     out = pl.pallas_call(
         kernel,
         out_shape=jax.ShapeDtypeStruct((pixels, CH), BF16),
-        in_specs=[pl.BlockSpec(memory_space=pltpu.VMEM)] * 8,
+        in_specs=[pl.BlockSpec(memory_space=pltpu.HBM)] * 8,
         out_specs=pl.BlockSpec(memory_space=pltpu.VMEM),
         scratch_shapes=[
+            pltpu.VMEM((pixels, CH), BF16),
+            pltpu.VMEM((6, CH, CH), BF16),
+            pltpu.VMEM((1, CH), F32),
             pltpu.VMEM((128 * WIDE, CH), F32),
             pltpu.VMEM((4 * CH, CH), BF16),
             pltpu.VMEM((CH, CH), F32),
-            pltpu.VMEM((2, CH * WIDE, CH), F32),
+            pltpu.VMEM((CH * WIDE, CH), F32),
+            pltpu.VMEM((CH * WIDE, CH), F32),
             pltpu.VMEM((2, ROWS, COLS, CHUNK, CH), BF16),
             pltpu.VMEM((2, ROWS, COLS, CHUNK, CH), BF16),
             pltpu.VMEM((2, COLS, CHUNK, 384), BF16),
@@ -348,14 +390,15 @@
             pltpu.VMEM((ROWS, COLS, CHUNK, CH), BF16),
             pltpu.VMEM((pixels, CH), F32),
             pltpu.VMEM((2, WIDE, CH), F32),
-            dma((2, subs, 3)), dma((2, subs, 3)),
+            dma((8,)),
+            dma((2, 4, 3)), dma((2, 4, 3)),
             dma((2, 14)), dma((2, 14)),
             dma((2, 8)), dma((2, 8)),
             dma((14,)), dma((14,)),
             dma((subs, 3)), dma((subs, 3)),
         ],
         compiler_params=pltpu.CompilerParams(
-            collective_id=0, has_side_effects=True, vmem_limit_bytes=48 * 1024 * 1024
+            collective_id=0, has_side_effects=True, vmem_limit_bytes=67043328
         ),
     )(
         pair_rows.reshape(pixels, CH),

time: 120 us -> 105 us (0.88)
  Pallas kernels: 112 us -> 102 us
  local copies, waits for them, and re-layouts: 7.08 us -> 1.94 us
    pallas_call x1, Pallas kernels: 112 us -> 102 us  [per_device(): pl.pallas_call(kernel, out_shape=jax.ShapeDtypeStruct((pixels, CH), BF16)...]
    unnamed x17 -> x1, local copies, waits for them, and re-layouts: 7.08 us -> 1.94 us
where the time goes in v2:
time: 105 us; the launch traced here: 104 us
  Pallas kernels  102 us (97%)
  local copies, waits for them, and re-layouts  1.94 us (2%)
    pallas_call x1, Pallas kernels, per_device(): pl.pallas_call(kernel, out_shape=jax.ShapeDtypeStruct((pixels, CH), BF16)...  102 us

profile of v2, /device:TPU:6, one launch (start us, length us, event | category | flops | bytes accessed | tf_op | source)
XLA Modules:
  0.0 103.5 jit_solution(6853200128231731155)
XLA Ops:
  0.0 101.6 %shard_map.82 = bf16[2304,128]{1,0:T(8,128)(2,1)} custom-call(bf16[2304,128]{1,0:T(8,128)(2,1)} %bitcast.4, bf16[128,128]{1,0:T(8,128)(2,1)} %lw_hbm.1, bf16[128,128]{1,0:T(8,128)(2,1)} %lg_hbm.1, bf16[128,128]{1,0:T(8,128)(2,1)} %rw_hbm.1, bf16[128,128]{1,0:T(8,128)(2,1)} %rg_hbm.1, f32[1,128]{1,0:T(1,128)} %bitcast.5, bf16[128,128]{1,0:T(8,128)(2,1)} %ow_hbm.1, ...), custom_call_target="tpu_custom_call" | custom-call | tf_op jit(solution)/shard_map/pallas_call | solution.py:366
  101.6 1.9 %copy.10 = bf16[96,24,128]{2,1,0:T(8,128)(2,1)} copy(bf16[96,24,128]{2,1,0:T(8,128)(2,1)} %bitcast.3) | data formatting | bytes 1179648

commit v3 on v2

v3 whole, which is shorter than its diff:
```python
import functools

import jax
import jax.numpy as jnp
from jax import lax
from jax.experimental import pallas as pl
from jax.experimental.pallas import tpu as pltpu
from jax.sharding import PartitionSpec as P

MESH = pl.DeviceIdType.MESH
F32, BF16 = jnp.float32, jnp.bfloat16
ROWS, COLS = 4, 16
LINES, WIDE, CH = 96, 24, 128
TEAM = 4
FAR = (COLS - TEAM) // 2
CHUNK = 2 * WIDE
if TEAM == 4:
    YSUBS = (((0, 2), (2, 6), (6, 12), (12, 16)), ((12, 16), (8, 12), (4, 8), (2, 4), (0, 2)))
    ESUBS = ((12, 16), (10, 12), (6, 10), (4, 6), (2, 4), (0, 2))
else:
    YSUBS = (((0, 2), (2, 6), (6, 14), (14, 16)), ((14, 16), (8, 14), (4, 8), (2, 4), (0, 2)))
    ESUBS = ((14, 16), (12, 14), (8, 12), (6, 8), (4, 6), (2, 4), (0, 2))


def sigmoid(x):
    return 0.5 + 0.5 * jnp.tanh(0.5 * x)


def nt(a, b):
    return lax.dot_general(a, b, (((1,), (1,)), ((), ())), preferred_element_type=F32)


def kernel(
    x_hbm, lw_hbm, lg_hbm, rw_hbm, rg_hbm, gain_hbm, ow_hbm, og_hbm,
    o_ref,
    x_ref, wraw, gain_ref, xf, xr, wf, wt, gb, facl, facr, fac0, zs, yb, zb, lb, rb, ri, lm, rm,
    cs, cb, es, ds, gt, stat,
    insem, ysend, yrecv, zsend, zrecv, xsend, xrecv, csend, crecv, esend, erecv,
):
    y = lax.axis_index("row")
    z = lax.axis_index("col")

    def row_at(o):
        return lax.rem(y + o, ROWS)

    def col_at(s):
        return lax.rem(z + s + COLS, COLS)

    steps = [(s, way) for s in range(FAR, 0, -1) for way in (0, 1)]

    mats = (lw_hbm, lg_hbm, rw_hbm, rg_hbm, ow_hbm, og_hbm)
    loads = [pltpu.make_async_copy(m, wraw.at[n], insem.at[n]) for n, m in enumerate(mats)]
    loads += [pltpu.make_async_copy(gain_hbm, gain_ref, insem.at[6])]
    third = LINES * WIDE // 3
    loads += [
        pltpu.make_async_copy(
            x_hbm.at[pl.ds(third * n, third)], x_ref.at[pl.ds(third * n, third)], insem.at[7 + n]
        )
        for n in range(3)
    ]
    for load in loads:
        load.start()

    barrier = pltpu.get_barrier_semaphore()
    for o in range(1, ROWS):
        pl.semaphore_signal(barrier, inc=1, device_id={"row": row_at(o)}, device_id_type=MESH)
    for s, way in steps:
        pl.semaphore_signal(
            barrier, inc=1, device_id={"col": col_at(s if way == 0 else -s)}, device_id_type=MESH
        )

    def team_of(t, own):
        if own:
            return lax.rem(z + COLS - (t - 2 * FAR), COLS)
        s = FAR - t // 2
        way = t % 2
        return lax.rem(z + COLS + (1 - 2 * way) * s - (TEAM - 1) * way, COLS)

    facs = (facl, facr)

    xf[pl.ds(LINES * WIDE, 32 * WIDE), :] = jnp.zeros((32 * WIDE, CH), F32)
    for load in loads[:7]:
        load.wait()
    for n in range(4):
        turned = wraw[n].astype(F32).T
        if n < 2:
            wf[pl.ds(CH * n, CH), :] = turned
        wt[pl.ds(CH * n, CH), :] = turned.astype(BF16)
    gb[...] = jnp.broadcast_to(gain_ref[...], (CH, CH)).T
    picks = []
    for n in range(2):
        for t in range(2):
            for ph in range(2):
                picks.append(wf[pl.ds(CH * n + 2 * team_of(t, False) + ph, ROWS, stride=32), :])
    first_w = jnp.concatenate(picks, axis=0).astype(BF16)
    for n in range(3):
        loads[7 + n].wait()
        xf[pl.ds(third * n, third), :] = x_ref[pl.ds(third * n, third), :].astype(F32)

    @pl.loop(0, WIDE // 2, unroll=3)
    def _(n):
        parts = []
        for i in (2 * n, 2 * n + 1):
            for b in range(4):
                block = lax.rem(b + y, 4)
                parts.append(xf[pl.ds(block * (32 * WIDE) + i, 32, stride=WIDE), :])
        xi = jnp.concatenate(parts, axis=0).astype(BF16)
        xr[pl.ds(pl.multiple_of(2 * CH * n, 2 * CH), 2 * CH), :] = xi
        both = nt(first_w, xi)
        value = both[:16] * sigmoid(both[16:])
        for m in range(2):
            fac0[pl.ds(2 * n + m, 16, stride=WIDE), :] = value[:, CH * m : CH * m + CH]

    def project(arr):
        @pl.loop(0, WIDE // 2, unroll=3)
        def _(n):
            xi = xr[pl.ds(pl.multiple_of(2 * CH * n, 2 * CH), 2 * CH), :]
            both = nt(wt[pl.ds(2 * CH * arr, 2 * CH), :], xi)
            value = both[:CH] * sigmoid(both[CH:])
            for m in range(2):
                facs[arr][pl.ds(2 * n + m, CH, stride=WIDE), :] = value[:, CH * m : CH * m + CH]

    def y_copy(arr, sub, o):
        t0, t1 = YSUBS[arr][sub]
        dest = row_at(o)
        return pltpu.make_async_remote_copy(
            src_ref=zs.at[arr, dest, pl.ds(t0, t1 - t0)],
            dst_ref=yb.at[arr, y, pl.ds(t0, t1 - t0)],
            send_sem=ysend.at[arr, sub, o - 1],
            recv_sem=yrecv.at[arr, sub, o - 1],
            device_id={"row": dest},
            device_id_type=MESH,
        )

    def over_row(arr, sub):
        t0, t1 = YSUBS[arr][sub]

        @pl.loop(t0, t1)
        def _(t):
            team = team_of(t, t0 >= 2 * FAR)
            for q in range(ROWS):
                first = pl.multiple_of((32 * q + 2 * team) * WIDE, 16)
                zs[arr, q, t] = facs[arr][pl.ds(first, CHUNK), :].astype(BF16)
            first = pl.multiple_of((32 * y + 2 * team) * WIDE, 16)
            yb[arr, y, t] = facs[arr][pl.ds(first, CHUNK), :].astype(BF16)

        for o in range(1, ROWS):
            y_copy(arr, sub, o).start()

    def z_copy(arr, s, way):
        t = 2 * (FAR - s) + way
        dst = lb.at[(TEAM - 1) * way, z] if arr == 0 else rb.at[way, s]
        return pltpu.make_async_remote_copy(
            src_ref=zb.at[arr, t],
            dst_ref=dst,
            send_sem=zsend.at[arr, t],
            recv_sem=zrecv.at[arr, t],
            device_id={"col": col_at(s if way == 0 else -s)},
            device_id_type=MESH,
        )

    lane = lax.broadcasted_iota(jnp.int32, (CHUNK, CH), 1)

    def join(arr, t):
        a, b, c, d = (yb[arr, q, t].astype(F32) for q in range(ROWS))
        return jnp.concatenate(
            [
                jnp.where(lane < 96, a, b),
                jnp.where(lane < 64, b, c),
                jnp.where(lane < 32, c, d),
            ],
            axis=1,
        ).astype(BF16)

    def over_col(arr, sub):
        t0, t1 = YSUBS[arr][sub]
        for o in range(1, ROWS):
            y_copy(arr, sub, o).wait_recv()
        if t0 >= 2 * FAR:
            for e in range(TEAM):
                if arr == 0:
                    lb[e, z] = join(arr, t0 + e)
                elif e in (0, TEAM - 1):
                    rb[e // (TEAM - 1), 0] = join(arr, t0 + e)
                else:
                    ri[e - 1] = join(arr, t0 + e)
            return

        @pl.loop(t0, t1)
        def _(t):
            zb[arr, t] = join(arr, t)

        sends = list(range(t0, t1))
        for t in sends if arr == 0 else sends[::-1]:
            z_copy(arr, FAR - t // 2, t % 2).start()

    def x_copy(way, r, s):
        src = col_at(-s if way == 0 else s)
        e = r if way == 0 else TEAM - 1 - r
        return pltpu.make_async_remote_copy(
            src_ref=lb.at[e, src],
            dst_ref=lb.at[e + 1 - 2 * way, src],
            send_sem=xsend.at[way, r, s],
            recv_sem=xrecv.at[way, r, s],
            device_id={"col": col_at(1 if way == 0 else -1)},
            device_id_type=MESH,
        )

    def gates():
        @pl.loop(0, 6)
        def _(n):
            rows = pl.ds(pl.multiple_of(n * 384, 384), 384)
            g = jnp.dot(x_ref[rows, :], wraw[5], preferred_element_type=F32)
            gt[rows, :] = sigmoid(g)

    for t in range(2):
        for q in range(ROWS):
            rows = [((2 * t + ph) * ROWS + q) * WIDE for ph in range(2)]
            zs[0, q, t] = jnp.concatenate(
                [fac0[pl.ds(first, WIDE), :] for first in rows], axis=0
            ).astype(BF16)
        rows = [pl.multiple_of(((2 * t + ph) * ROWS + y) * WIDE, 8) for ph in range(2)]
        yb[0, y, t] = jnp.concatenate(
            [fac0[pl.ds(first, WIDE), :] for first in rows], axis=0
        ).astype(BF16)
    pl.semaphore_wait(barrier, ROWS - 1 + len(steps))
    for o in range(1, ROWS):
        y_copy(0, 0, o).start()

    project(0)
    over_row(0, 1)
    over_row(0, 2)
    over_col(0, 0)
    over_row(0, 3)
    project(1)
    over_col(0, 1)
    over_row(1, 0)
    over_row(1, 1)
    over_col(0, 2)
    over_row(1, 2)
    over_row(1, 3)
    over_row(1, 4)
    over_col(0, 3)
    over_col(1, 0)
    over_col(1, 1)

    for way in (0, 1):
        for r in range(TEAM - 1):
            x_copy(way, r, 0).start()
    gates()
    for s, way in steps:
        z_copy(0, s, way).wait_recv()
        x_copy(way, 0, s).start()
    over_col(1, 2)
    for r in range(1, TEAM - 1):
        order = [1] + list(range(FAR + r, 1, -1)) if r == 1 else [1, 2] + list(range(FAR + r, 2, -1))
        for s in order:
            for way in (0, 1):
                x_copy(way, r - 1, s - 1).wait_recv()
                x_copy(way, r, s).start()
        if r == 1:
            over_col(1, 3)
    if TEAM == 2:
        over_col(1, 3)
    over_col(1, 4)

    def near_blocks(half):
        last = min(4 * half + 4, FAR + 1)
        for s in range(4 * half, last):
            if s:
                for way in (0, 1):
                    z_copy(1, s, way).wait_recv()
        for way in (0, 1):
            for s in range(4 * half, last, 2):
                one = rb[way, s].astype(F32)
                two = rb[way, s + 1].astype(F32) if s + 1 < last else one
                for ph in (0, 1):
                    cut = slice(WIDE * ph, WIDE * ph + WIDE)
                    rm[way, ph, pl.ds(WIDE * s, CHUNK), :] = jnp.concatenate(
                        [one[cut], two[cut]], axis=0
                    ).astype(BF16)

    def left_lines(e):
        for q in range(ROWS):
            four = [lb[e, 4 * q + n].astype(F32) for n in range(4)]
            for ph in (0, 1):
                cut = slice(WIDE * ph, WIDE * ph + WIDE)
                lines = jnp.concatenate([f[cut] for f in four], axis=0).astype(BF16)
                for u in range(3):
                    lm[e, ph, pl.ds(128 * u + 32 * ((q + u) % 4), 32), :] = lines[
                        32 * u : 32 * u + 32
                    ]

    def c_copy(s, way):
        t = 2 * (FAR - s) + way
        return pltpu.make_async_remote_copy(
            src_ref=cs.at[t],
            dst_ref=cb.at[t],
            send_sem=csend.at[t],
            recv_sem=crecv.at[t],
            device_id={"col": col_at(-s if way == 0 else s)},
            device_id_type=MESH,
        )

    scale = (ROWS * LINES) ** -0.5
    for e in range(1, TEAM - 1):
        left_lines(e)
        own = ri[e - 1].astype(F32)
        sums = [
            nt(own[WIDE * ph : WIDE * ph + WIDE].astype(BF16), lm[e, ph]) * scale for ph in (0, 1)
        ]
        cb[2 * FAR + e] = jnp.concatenate(sums, axis=0).astype(BF16)
    near_blocks(0)
    for way in (0, 1):
        r = TEAM - 2
        for s in range(FAR + r + 1):
            x_copy(1 - way, r, s).wait_recv()
        left_lines((TEAM - 1) * way)

    for half in (0, 1):
        if half:
            near_blocks(1)
        count = min(4, FAR + 1 - 4 * half)
        for way in (0, 1):
            e = (TEAM - 1) * way
            rows = pl.ds(96 * half, WIDE * count)
            sums = [nt(rm[way, ph, rows, :], lm[e, ph]) * scale for ph in (0, 1)]
            for n in range(count):
                s = 4 * half + n
                cut = slice(WIDE * n, WIDE * n + WIDE)
                chunk = jnp.concatenate([sums[0][cut], sums[1][cut]], axis=0).astype(BF16)
                if s == 0:
                    cb[2 * FAR + e] = chunk
                else:
                    cs[2 * (FAR - s) + way] = chunk
        for n in range(count):
            s = 4 * half + n
            for way in (0, 1):
                if s:
                    c_copy(s, way).start()

    def e_copy(sub, o):
        t0, t1 = ESUBS[sub]
        dest = row_at(o)
        return pltpu.make_async_remote_copy(
            src_ref=es.at[dest, pl.ds(t0, t1 - t0)],
            dst_ref=ds.at[y, pl.ds(t0, t1 - t0)],
            send_sem=esend.at[sub, o - 1],
            recv_sem=erecv.at[sub, o - 1],
            device_id={"row": dest},
            device_id_type=MESH,
        )

    strip = lane // 32

    for sub, (t0, t1) in enumerate(ESUBS):
        for t in range(t0, t1 if t0 < 2 * FAR else t0):
            c_copy(FAR - t // 2, t % 2).wait_recv()

        @pl.loop(t0, t1)
        def _(t):
            a, b, c = (cb[t, :, pl.ds(128 * u, 128)].astype(F32) for u in range(3))

            def quarter(q):
                return jnp.where(
                    strip == q, a, jnp.where(strip == lax.rem(q + 1, 4), b, c)
                ).astype(BF16)

            for q in range(ROWS):
                es[q, t] = quarter(q)
            ds[y, t] = quarter(y)

        for o in range(1, ROWS):
            e_copy(sub, o).start()

    mixed = facl
    total = jnp.zeros((WIDE, CH), F32)
    for sub, (t0, t1) in enumerate(ESUBS):
        for o in range(1, ROWS):
            e_copy(sub, o).wait_recv()

        def add(t, total, t0=t0):
            team = team_of(t, t0 >= 2 * FAR)
            for q in range(ROWS):
                block = ds[q, t].astype(F32)
                first = pl.multiple_of((32 * q + 2 * team) * WIDE, 16)
                mixed[pl.ds(first, CHUNK), :] = block
                total = total + block[:WIDE] + block[WIDE:]
            return total

        total = lax.fori_loop(t0, t1, add, total)
    mean = total * (1.0 / CH)

    def spread(n, total):
        for m in range(8):
            off = mixed[pl.ds(pl.multiple_of((8 * n + m) * WIDE, 8), WIDE), :] - mean
            total = total + off * off
        return total

    var = lax.fori_loop(0, CH // 8, spread, jnp.zeros((WIDE, CH), F32)) * (1.0 / CH)
    stat[0] = mean
    stat[1] = lax.rsqrt(var + 1e-05)

    out = facr

    @pl.loop(0, WIDE // 4)
    def _(n):
        scaled = []
        for j in range(4):
            block = mixed[pl.ds(4 * n + j, CH, stride=WIDE), :]
            block = (block - stat[0, pl.ds(4 * n + j, 1), :]) * stat[1, pl.ds(4 * n + j, 1), :] * gb[...]
            scaled.append(block.astype(BF16).T)
        change = jnp.dot(jnp.concatenate(scaled, axis=0), wraw[4], preferred_element_type=F32)
        for j in range(4):
            for b in range(4):
                u = lax.rem(b - y + 4, 4)
                out[pl.ds(u * (32 * WIDE) + 4 * n + j, 32, stride=WIDE), :] = change[
                    CH * j + 32 * b : CH * j + 32 * b + 32
                ]

    @pl.loop(0, 6)
    def _(n):
        rows = pl.ds(pl.multiple_of(n * 384, 384), 384)
        o_ref[rows, :] = (out[rows, :] * gt[rows, :]).astype(BF16)

    for arr in (0, 1):
        for sub in range(len(YSUBS[arr])):
            for o in range(1, ROWS):
                y_copy(arr, sub, o).wait_send()
        for s, way in steps:
            z_copy(arr, s, way).wait_send()
    for way in (0, 1):
        for r in range(TEAM - 1):
            for s in range(FAR + r + 1):
                x_copy(way, r, s).wait_send()
    for s, way in steps:
        c_copy(s, way).wait_send()
    for sub in range(len(ESUBS)):
        for o in range(1, ROWS):
            e_copy(sub, o).wait_send()


def per_device(
    pair_rows, left_weight, right_weight, left_gate, right_gate, mid_gain, out_weight, out_gate
):
    pixels = pair_rows.shape[0] * pair_rows.shape[1]
    dma = pltpu.SemaphoreType.DMA
    out = pl.pallas_call(
        kernel,
        out_shape=jax.ShapeDtypeStruct((pixels, CH), BF16),
        in_specs=[pl.BlockSpec(memory_space=pltpu.HBM)] * 8,
        out_specs=pl.BlockSpec(memory_space=pltpu.VMEM),
        scratch_shapes=[
            pltpu.VMEM((pixels, CH), BF16),
            pltpu.VMEM((6, CH, CH), BF16),
            pltpu.VMEM((1, CH), F32),
            pltpu.VMEM((128 * WIDE, CH), F32),
            pltpu.VMEM((128 * WIDE, CH), BF16),
            pltpu.VMEM((2 * CH, CH), F32),
            pltpu.VMEM((4 * CH, CH), BF16),
            pltpu.VMEM((CH, CH), F32),
            pltpu.VMEM((CH * WIDE, CH), F32),
            pltpu.VMEM((CH * WIDE, CH), F32),
            pltpu.VMEM((16 * WIDE, CH), F32),
            pltpu.VMEM((2, ROWS, COLS, CHUNK, CH), BF16),
            pltpu.VMEM((2, ROWS, COLS, CHUNK, CH), BF16),
            pltpu.VMEM((2, 2 * FAR, CHUNK, 384), BF16),
            pltpu.VMEM((TEAM, COLS, CHUNK, 384), BF16),
            pltpu.VMEM((2, FAR + 1, CHUNK, 384), BF16),
            pltpu.VMEM((2, CHUNK, 384), BF16),
            pltpu.VMEM((TEAM, 2, 384, 384), BF16),
            pltpu.VMEM((2, 2, 192, 384), BF16),
            pltpu.VMEM((2 * FAR, CHUNK, 384), BF16),
            pltpu.VMEM((COLS, CHUNK, 384), BF16),
            pltpu.VMEM((ROWS, COLS, CHUNK, CH), BF16),
            pltpu.VMEM((ROWS, COLS, CHUNK, CH), BF16),
            pltpu.VMEM((pixels, CH), F32),
            pltpu.VMEM((2, WIDE, CH), F32),
            dma((10,)),
            dma((2, 5, 3)), dma((2, 5, 3)),
            dma((2, 2 * FAR)), dma((2, 2 * FAR)),
            dma((2, TEAM - 1, COLS)), dma((2, TEAM - 1, COLS)),
            dma((2 * FAR,)), dma((2 * FAR,)),
            dma((len(ESUBS), 3)), dma((len(ESUBS), 3)),
        ],
        compiler_params=pltpu.CompilerParams(
            collective_id=0, has_side_effects=True, vmem_limit_bytes=48 * 1024 * 1024
        ),
    )(
        *[
            pltpu.with_memory_space_constraint(v, pltpu.HBM)
            for v in (
                pair_rows.reshape(pixels, CH),
                left_weight, left_gate, right_weight, right_gate,
                mid_gain.reshape(1, CH), out_weight, out_gate,
            )
        ]
    )
    return out.reshape(pair_rows.shape)


def solution(mesh):
    placed = (
        P(("trial", "row"), "col", None),
        P("trial", None),
        P("trial", None),
        P("trial", None),
        P("trial", None),
        P(),
        P("trial", None),
        P("trial", None),
    )
    return jax.shard_map(
        per_device,
        mesh=mesh,
        in_specs=placed,
        out_specs=P(("trial", "row"), "col", None),
        check_vma=False,
    )
```

time: 105 us -> 100 us (0.952); the launches traced: 104 us -> 100 us
  Pallas kernels: 102 us -> 99.5 us
  local copies, waits for them, and re-layouts: 1.94 us -> 0.82 us
    pallas_call x1, Pallas kernels: 102 us -> 99.5 us  [per_device(): pl.pallas_call(kernel, out_shape=jax.ShapeDtypeStruct((pixels, CH), BF16)...]
    unnamed x1, local copies, waits for them, and re-layouts: 1.94 us -> 0.82 us
where the time goes in v3:
time: 100 us
  Pallas kernels  99.5 us (100%)
    pallas_call x1, Pallas kernels, per_device(): pl.pallas_call(kernel, out_shape=jax.ShapeDtypeStruct((pixels, CH), BF16)...  99.5 us

profile of v3, /device:TPU:6, one launch (start us, length us, event | category | flops | bytes accessed | tf_op | source)
XLA Modules:
  0.0 100.4 jit_solution(6421408306845541)
XLA Ops:
  0.0 99.5 %shard_map.82 = bf16[2304,128]{1,0:T(8,128)(2,1)S(1)} custom-call(bf16[2304,128]{1,0:T(8,128)(2,1)} %bitcast.4, bf16[128,128]{1,0:T(8,128)(2,1)} %lw_hbm.1, bf16[128,128]{1,0:T(8,128)(2,1)} %lg_hbm.1, bf16[128,128]{1,0:T(8,128)(2,1)} %rw_hbm.1, bf16[128,128]{1,0:T(8,128)(2,1)} %rg_hbm.1, f32[1,128]{1,0:T(1,128)} %bitcast.5, bf16[128,128]{1,0:T(8,128)(2,1)} %ow_hbm.1, ...), custom_call_target="tpu_custom_call" | custom-call | tf_op jit(solution)/shard_map/pallas_call | solution.py:448
  99.5 0.8 copy.10

commit v4 on v3

--- a/solution.py
+++ b/solution.py
@@ -14,12 +14,9 @@
 TEAM = 4
 FAR = (COLS - TEAM) // 2
 CHUNK = 2 * WIDE
-if TEAM == 4:
-    YSUBS = (((0, 2), (2, 6), (6, 12), (12, 16)), ((12, 16), (8, 12), (4, 8), (2, 4), (0, 2)))
-    ESUBS = ((12, 16), (10, 12), (6, 10), (4, 6), (2, 4), (0, 2))
-else:
-    YSUBS = (((0, 2), (2, 6), (6, 14), (14, 16)), ((14, 16), (8, 14), (4, 8), (2, 4), (0, 2)))
-    ESUBS = ((14, 16), (12, 14), (8, 12), (6, 8), (4, 6), (2, 4), (0, 2))
+YSUBS = (((0, 2), (2, 6), (6, 12), (12, 16)), ((12, 16), (10, 12), (0, 2), (2, 4), (4, 10)))
+ESUBS = ((12, 16), (10, 12), (0, 2), (2, 4), (4, 6), (6, 8), (8, 10))
+HALVES = ((0, 1, 6, 5), (4, 3, 2))
 
 
 def sigmoid(x):
@@ -35,7 +32,7 @@
     o_ref,
     x_ref, wraw, gain_ref, xf, xr, wf, wt, gb, facl, facr, fac0, zs, yb, zb, lb, rb, ri, lm, rm,
     cs, cb, es, ds, gt, stat,
-    insem, ysend, yrecv, zsend, zrecv, xsend, xrecv, csend, crecv, esend, erecv,
+    insem, sent, yrecv, zrecv, xrecv, crecv, erecv,
 ):
     y = lax.axis_index("row")
     z = lax.axis_index("col")
@@ -49,17 +46,23 @@
     steps = [(s, way) for s in range(FAR, 0, -1) for way in (0, 1)]
 
     mats = (lw_hbm, lg_hbm, rw_hbm, rg_hbm, ow_hbm, og_hbm)
-    loads = [pltpu.make_async_copy(m, wraw.at[n], insem.at[n]) for n, m in enumerate(mats)]
-    loads += [pltpu.make_async_copy(gain_hbm, gain_ref, insem.at[6])]
-    third = LINES * WIDE // 3
-    loads += [
-        pltpu.make_async_copy(
-            x_hbm.at[pl.ds(third * n, third)], x_ref.at[pl.ds(third * n, third)], insem.at[7 + n]
-        )
-        for n in range(3)
-    ]
+    loads = [pltpu.make_async_copy(m, wraw.at[n], insem.at[0]) for n, m in enumerate(mats)]
+    loads += [pltpu.make_async_copy(gain_hbm, gain_ref, insem.at[1])]
+    loads += [pltpu.make_async_copy(x_hbm, x_ref, insem.at[2])]
     for load in loads:
         load.start()
+
+    def arrived(ref, sem):
+        pltpu.make_async_remote_copy(
+            src_ref=ref, dst_ref=ref, send_sem=sem, recv_sem=sem,
+            device_id={"col": col_at(1)}, device_id_type=MESH,
+        ).wait_recv()
+
+    def departed(ref, sem):
+        pltpu.make_async_remote_copy(
+            src_ref=ref, dst_ref=ref, send_sem=sem, recv_sem=sem,
+            device_id={"col": col_at(1)}, device_id_type=MESH,
+        ).wait_send()
 
     barrier = pltpu.get_barrier_semaphore()
     for o in range(1, ROWS):
@@ -79,8 +82,8 @@
     facs = (facl, facr)
 
     xf[pl.ds(LINES * WIDE, 32 * WIDE), :] = jnp.zeros((32 * WIDE, CH), F32)
-    for load in loads[:7]:
-        load.wait()
+    pltpu.make_async_copy(wraw, wraw, insem.at[0]).wait()
+    loads[6].wait()
     for n in range(4):
         turned = wraw[n].astype(F32).T
         if n < 2:
@@ -93,9 +96,8 @@
             for ph in range(2):
                 picks.append(wf[pl.ds(CH * n + 2 * team_of(t, False) + ph, ROWS, stride=32), :])
     first_w = jnp.concatenate(picks, axis=0).astype(BF16)
-    for n in range(3):
-        loads[7 + n].wait()
-        xf[pl.ds(third * n, third), :] = x_ref[pl.ds(third * n, third), :].astype(F32)
+    loads[7].wait()
+    xf[pl.ds(0, LINES * WIDE), :] = x_ref[...].astype(F32)
 
     @pl.loop(0, WIDE // 2, unroll=3)
     def _(n):
@@ -126,8 +128,8 @@
         return pltpu.make_async_remote_copy(
             src_ref=zs.at[arr, dest, pl.ds(t0, t1 - t0)],
             dst_ref=yb.at[arr, y, pl.ds(t0, t1 - t0)],
-            send_sem=ysend.at[arr, sub, o - 1],
-            recv_sem=yrecv.at[arr, sub, o - 1],
+            send_sem=sent.at[0],
+            recv_sem=yrecv.at[4 * arr + sub],
             device_id={"row": dest},
             device_id_type=MESH,
         )
@@ -153,8 +155,8 @@
         return pltpu.make_async_remote_copy(
             src_ref=zb.at[arr, t],
             dst_ref=dst,
-            send_sem=zsend.at[arr, t],
-            recv_sem=zrecv.at[arr, t],
+            send_sem=sent.at[1],
+            recv_sem=zrecv.at[(s - 1) // 2 if arr == 0 else 3 if s in HALVES[0] else 4],
             device_id={"col": col_at(s if way == 0 else -s)},
             device_id_type=MESH,
         )
@@ -174,8 +176,7 @@
 
     def over_col(arr, sub):
         t0, t1 = YSUBS[arr][sub]
-        for o in range(1, ROWS):
-            y_copy(arr, sub, o).wait_recv()
+        arrived(yb.at[arr, pl.ds(0, 3), pl.ds(t0, t1 - t0)], yrecv.at[4 * arr + sub])
         if t0 >= 2 * FAR:
             for e in range(TEAM):
                 if arr == 0:
@@ -190,8 +191,7 @@
         def _(t):
             zb[arr, t] = join(arr, t)
 
-        sends = list(range(t0, t1))
-        for t in sends if arr == 0 else sends[::-1]:
+        for t in range(t0, t1):
             z_copy(arr, FAR - t // 2, t % 2).start()
 
     def x_copy(way, r, s):
@@ -200,8 +200,8 @@
         return pltpu.make_async_remote_copy(
             src_ref=lb.at[e, src],
             dst_ref=lb.at[e + 1 - 2 * way, src],
-            send_sem=xsend.at[way, r, s],
-            recv_sem=xrecv.at[way, r, s],
+            send_sem=sent.at[2],
+            recv_sem=xrecv.at[((s + 1) // 2, 4 + s // 2, 8)[r]],
             device_id={"col": col_at(1 if way == 0 else -1)},
             device_id_type=MESH,
         )
@@ -244,39 +244,43 @@
     over_col(1, 0)
     over_col(1, 1)
 
+    over_col(1, 2)
+
     for way in (0, 1):
         for r in range(TEAM - 1):
             x_copy(way, r, 0).start()
     gates()
-    for s, way in steps:
-        z_copy(0, s, way).wait_recv()
-        x_copy(way, 0, s).start()
-    over_col(1, 2)
-    for r in range(1, TEAM - 1):
-        order = [1] + list(range(FAR + r, 1, -1)) if r == 1 else [1, 2] + list(range(FAR + r, 2, -1))
-        for s in order:
+    pairs = ((6, 5), (4, 3), (2, 1))
+    for pair in pairs:
+        arrived(zb.at[0, pl.ds(0, 4)], zrecv.at[(pair[1] - 1) // 2])
+        for s in pair:
             for way in (0, 1):
-                x_copy(way, r - 1, s - 1).wait_recv()
-                x_copy(way, r, s).start()
-        if r == 1:
-            over_col(1, 3)
-    if TEAM == 2:
-        over_col(1, 3)
+                x_copy(way, 0, s).start()
+    over_col(1, 3)
+    arrived(zb.at[0, pl.ds(0, 2)], xrecv.at[0])
+    for way in (0, 1):
+        x_copy(way, 1, 1).start()
+    for pair in pairs:
+        arrived(zb.at[0, pl.ds(0, 4)], xrecv.at[(pair[1] + 1) // 2])
+        for s in pair:
+            for way in (0, 1):
+                x_copy(way, 1, s + 1).start()
+    for pair in ((1, 0), (7, 6), (5, 4), (3, 2)):
+        arrived(zb.at[0, pl.ds(0, 4)], xrecv.at[4 + pair[1] // 2])
+        for s in pair:
+            for way in (0, 1):
+                x_copy(way, 2, s + 1).start()
     over_col(1, 4)
 
     def near_blocks(half):
-        last = min(4 * half + 4, FAR + 1)
-        for s in range(4 * half, last):
-            if s:
-                for way in (0, 1):
-                    z_copy(1, s, way).wait_recv()
+        arrived(zb.at[0, pl.ds(0, 6)], zrecv.at[3 + half])
         for way in (0, 1):
-            for s in range(4 * half, last, 2):
-                one = rb[way, s].astype(F32)
-                two = rb[way, s + 1].astype(F32) if s + 1 < last else one
+            for n in range(0, len(HALVES[half]), 2):
+                one = rb[way, HALVES[half][n]].astype(F32)
+                two = rb[way, HALVES[half][min(n + 1, len(HALVES[half]) - 1)]].astype(F32)
                 for ph in (0, 1):
                     cut = slice(WIDE * ph, WIDE * ph + WIDE)
-                    rm[way, ph, pl.ds(WIDE * s, CHUNK), :] = jnp.concatenate(
+                    rm[way, ph, pl.ds(96 * half + WIDE * n, CHUNK), :] = jnp.concatenate(
                         [one[cut], two[cut]], axis=0
                     ).astype(BF16)
 
@@ -296,8 +300,8 @@
         return pltpu.make_async_remote_copy(
             src_ref=cs.at[t],
             dst_ref=cb.at[t],
-            send_sem=csend.at[t],
-            recv_sem=crecv.at[t],
+            send_sem=sent.at[3],
+            recv_sem=crecv.at[s - 1],
             device_id={"col": col_at(-s if way == 0 else s)},
             device_id_type=MESH,
         )
@@ -311,30 +315,26 @@
         ]
         cb[2 * FAR + e] = jnp.concatenate(sums, axis=0).astype(BF16)
     near_blocks(0)
+    arrived(zb.at[:, pl.ds(0, 9)], xrecv.at[8])
     for way in (0, 1):
-        r = TEAM - 2
-        for s in range(FAR + r + 1):
-            x_copy(1 - way, r, s).wait_recv()
         left_lines((TEAM - 1) * way)
 
     for half in (0, 1):
         if half:
             near_blocks(1)
-        count = min(4, FAR + 1 - 4 * half)
+        count = len(HALVES[half])
         for way in (0, 1):
             e = (TEAM - 1) * way
             rows = pl.ds(96 * half, WIDE * count)
             sums = [nt(rm[way, ph, rows, :], lm[e, ph]) * scale for ph in (0, 1)]
-            for n in range(count):
-                s = 4 * half + n
+            for n, s in enumerate(HALVES[half]):
                 cut = slice(WIDE * n, WIDE * n + WIDE)
                 chunk = jnp.concatenate([sums[0][cut], sums[1][cut]], axis=0).astype(BF16)
                 if s == 0:
                     cb[2 * FAR + e] = chunk
                 else:
                     cs[2 * (FAR - s) + way] = chunk
-        for n in range(count):
-            s = 4 * half + n
+        for s in HALVES[half]:
             for way in (0, 1):
                 if s:
                     c_copy(s, way).start()
@@ -345,8 +345,8 @@
         return pltpu.make_async_remote_copy(
             src_ref=es.at[dest, pl.ds(t0, t1 - t0)],
             dst_ref=ds.at[y, pl.ds(t0, t1 - t0)],
-            send_sem=esend.at[sub, o - 1],
-            recv_sem=erecv.at[sub, o - 1],
+            send_sem=sent.at[4],
+            recv_sem=erecv.at[sub],
             device_id={"row": dest},
             device_id_type=MESH,
         )
@@ -354,8 +354,8 @@
     strip = lane // 32
 
     for sub, (t0, t1) in enumerate(ESUBS):
-        for t in range(t0, t1 if t0 < 2 * FAR else t0):
-            c_copy(FAR - t // 2, t % 2).wait_recv()
+        if t0 < 2 * FAR:
+            arrived(zb.at[0, pl.ds(0, 2)], crecv.at[FAR - t0 // 2 - 1])
 
         @pl.loop(t0, t1)
         def _(t):
@@ -376,8 +376,7 @@
     mixed = facl
     total = jnp.zeros((WIDE, CH), F32)
     for sub, (t0, t1) in enumerate(ESUBS):
-        for o in range(1, ROWS):
-            e_copy(sub, o).wait_recv()
+        arrived(ds.at[pl.ds(0, 3), pl.ds(t0, t1 - t0)], erecv.at[sub])
 
         def add(t, total, t0=t0):
             team = team_of(t, t0 >= 2 * FAR)
@@ -423,21 +422,11 @@
         rows = pl.ds(pl.multiple_of(n * 384, 384), 384)
         o_ref[rows, :] = (out[rows, :] * gt[rows, :]).astype(BF16)
 
-    for arr in (0, 1):
-        for sub in range(len(YSUBS[arr])):
-            for o in range(1, ROWS):
-                y_copy(arr, sub, o).wait_send()
-        for s, way in steps:
-            z_copy(arr, s, way).wait_send()
-    for way in (0, 1):
-        for r in range(TEAM - 1):
-            for s in range(FAR + r + 1):
-                x_copy(way, r, s).wait_send()
-    for s, way in steps:
-        c_copy(s, way).wait_send()
-    for sub in range(len(ESUBS)):
-        for o in range(1, ROWS):
-            e_copy(sub, o).wait_send()
+    departed(zs.at[:, pl.ds(0, 3)], sent.at[0])
+    departed(zb, sent.at[1])
+    departed(lb.at[pl.ds(0, 3)], sent.at[2])
+    departed(cs, sent.at[3])
+    departed(es.at[pl.ds(0, 3)], sent.at[4])
 
 
 def per_device(
@@ -476,12 +465,7 @@
             pltpu.VMEM((ROWS, COLS, CHUNK, CH), BF16),
             pltpu.VMEM((pixels, CH), F32),
             pltpu.VMEM((2, WIDE, CH), F32),
-            dma((10,)),
-            dma((2, 5, 3)), dma((2, 5, 3)),
-            dma((2, 2 * FAR)), dma((2, 2 * FAR)),
-            dma((2, TEAM - 1, COLS)), dma((2, TEAM - 1, COLS)),
-            dma((2 * FAR,)), dma((2 * FAR,)),
-            dma((len(ESUBS), 3)), dma((len(ESUBS), 3)),
+            dma((3,)), dma((5,)), dma((9,)), dma((5,)), dma((9,)), dma((FAR,)), dma((len(ESUBS),)),
         ],
         compiler_params=pltpu.CompilerParams(
             collective_id=0, has_side_effects=True, vmem_limit_bytes=48 * 1024 * 1024

time: 100 us -> 95.8 us (0.958)
  Pallas kernels: 99.5 us -> 94.8 us
    pallas_call x1, Pallas kernels: 99.5 us -> 94.8 us  [per_device(): pl.pallas_call(kernel, out_shape=jax.ShapeDtypeStruct((pixels, CH), BF16)...]
where the time goes in v4:
time: 95.8 us; the launch traced here: 95.6 us
  Pallas kernels  94.8 us (99%)
    pallas_call x1, Pallas kernels, per_device(): pl.pallas_call(kernel, out_shape=jax.ShapeDtypeStruct((pixels, CH), BF16)...  94.8 us

profile of v4, /device:TPU:6, one launch (start us, length us, event | category | flops | bytes accessed | tf_op | source)
XLA Modules:
  0.0 95.6 jit_solution(1671495521231111643)
XLA Ops:
  0.0 94.8 %shard_map.82 = bf16[2304,128]{1,0:T(8,128)(2,1)S(1)} custom-call(bf16[2304,128]{1,0:T(8,128)(2,1)} %bitcast.4, bf16[128,128]{1,0:T(8,128)(2,1)} %lw_hbm.1, bf16[128,128]{1,0:T(8,128)(2,1)} %lg_hbm.1, bf16[128,128]{1,0:T(8,128)(2,1)} %rw_hbm.1, bf16[128,128]{1,0:T(8,128)(2,1)} %rg_hbm.1, f32[1,128]{1,0:T(1,128)} %bitcast.5, bf16[128,128]{1,0:T(8,128)(2,1)} %ow_hbm.1, ...), custom_call_target="tpu_custom_call" | custom-call | tf_op jit(solution)/shard_map/pallas_call | solution.py:437
  94.8 0.8 copy.10

commit v5 on v4

--- a/solution.py
+++ b/solution.py
@@ -11,12 +11,23 @@
 F32, BF16 = jnp.float32, jnp.bfloat16
 ROWS, COLS = 4, 16
 LINES, WIDE, CH = 96, 24, 128
-TEAM = 4
+TEAM = 6
 FAR = (COLS - TEAM) // 2
 CHUNK = 2 * WIDE
-YSUBS = (((0, 2), (2, 6), (6, 12), (12, 16)), ((12, 16), (10, 12), (0, 2), (2, 4), (4, 10)))
-ESUBS = ((12, 16), (10, 12), (0, 2), (2, 4), (4, 6), (6, 8), (8, 10))
-HALVES = ((0, 1, 6, 5), (4, 3, 2))
+YSUBS = (((0, 2), (2, 6), (6, 10), (10, 16)), ((10, 16), (8, 10), (0, 2), (2, 4), (4, 8)))
+ESUBS = ((10, 16), (8, 10), (0, 2), (2, 4), (4, 6), (6, 8))
+HALVES = ((0, 1, 5, 4), (3, 2))
+DIRECT = ((5,), (4, 3), (2, 1))
+ORDERS = [[0, 5, 4, 3, 2, 1]]
+while len(ORDERS) < TEAM - 1:
+    ORDERS.append([0] + [s + 1 for s in ORDERS[-1]])
+GROUPS = [[order[n : n + 2] for n in range(0, len(order), 2)] for order in ORDERS]
+GROUPS[-1] = [ORDERS[-1]]
+XBASE = [sum(len(g) for g in GROUPS[:r]) for r in range(TEAM)]
+
+
+def hand_sem(r, s):
+    return XBASE[r] + [s in group for group in GROUPS[r]].index(True)
 
 
 def sigmoid(x):
@@ -201,7 +212,7 @@
             src_ref=lb.at[e, src],
             dst_ref=lb.at[e + 1 - 2 * way, src],
             send_sem=sent.at[2],
-            recv_sem=xrecv.at[((s + 1) // 2, 4 + s // 2, 8)[r]],
+            recv_sem=xrecv.at[hand_sem(r, s)],
             device_id={"col": col_at(1 if way == 0 else -1)},
             device_id_type=MESH,
         )
@@ -250,30 +261,22 @@
         for r in range(TEAM - 1):
             x_copy(way, r, 0).start()
     gates()
-    pairs = ((6, 5), (4, 3), (2, 1))
-    for pair in pairs:
-        arrived(zb.at[0, pl.ds(0, 4)], zrecv.at[(pair[1] - 1) // 2])
-        for s in pair:
+    for near in DIRECT:
+        arrived(zb.at[0, pl.ds(0, 2 * len(near))], zrecv.at[(near[-1] - 1) // 2])
+        for s in near:
             for way in (0, 1):
                 x_copy(way, 0, s).start()
     over_col(1, 3)
-    arrived(zb.at[0, pl.ds(0, 2)], xrecv.at[0])
-    for way in (0, 1):
-        x_copy(way, 1, 1).start()
-    for pair in pairs:
-        arrived(zb.at[0, pl.ds(0, 4)], xrecv.at[(pair[1] + 1) // 2])
-        for s in pair:
-            for way in (0, 1):
-                x_copy(way, 1, s + 1).start()
-    for pair in ((1, 0), (7, 6), (5, 4), (3, 2)):
-        arrived(zb.at[0, pl.ds(0, 4)], xrecv.at[4 + pair[1] // 2])
-        for s in pair:
-            for way in (0, 1):
-                x_copy(way, 2, s + 1).start()
+    for r in range(1, TEAM - 1):
+        for n, group in enumerate(GROUPS[r - 1]):
+            arrived(zb.at[0, pl.ds(0, 2 * len(group))], xrecv.at[XBASE[r - 1] + n])
+            for s in group:
+                for way in (0, 1):
+                    x_copy(way, r, s + 1).start()
     over_col(1, 4)
 
     def near_blocks(half):
-        arrived(zb.at[0, pl.ds(0, 6)], zrecv.at[3 + half])
+        arrived(zb.at[0, pl.ds(0, 2 * sum(s > 0 for s in HALVES[half]))], zrecv.at[3 + half])
         for way in (0, 1):
             for n in range(0, len(HALVES[half]), 2):
                 one = rb[way, HALVES[half][n]].astype(F32)
@@ -315,7 +318,7 @@
         ]
         cb[2 * FAR + e] = jnp.concatenate(sums, axis=0).astype(BF16)
     near_blocks(0)
-    arrived(zb.at[:, pl.ds(0, 9)], xrecv.at[8])
+    arrived(zb, xrecv.at[XBASE[TEAM - 2]])
     for way in (0, 1):
         left_lines((TEAM - 1) * way)
 
@@ -424,7 +427,7 @@
 
     departed(zs.at[:, pl.ds(0, 3)], sent.at[0])
     departed(zb, sent.at[1])
-    departed(lb.at[pl.ds(0, 3)], sent.at[2])
+    departed(lb.at[pl.ds(0, TEAM - 1)], sent.at[2])
     departed(cs, sent.at[3])
     departed(es.at[pl.ds(0, 3)], sent.at[4])
 
@@ -456,7 +459,7 @@
             pltpu.VMEM((2, 2 * FAR, CHUNK, 384), BF16),
             pltpu.VMEM((TEAM, COLS, CHUNK, 384), BF16),
             pltpu.VMEM((2, FAR + 1, CHUNK, 384), BF16),
-            pltpu.VMEM((2, CHUNK, 384), BF16),
+            pltpu.VMEM((TEAM - 2, CHUNK, 384), BF16),
             pltpu.VMEM((TEAM, 2, 384, 384), BF16),
             pltpu.VMEM((2, 2, 192, 384), BF16),
             pltpu.VMEM((2 * FAR, CHUNK, 384), BF16),
@@ -465,7 +468,7 @@
             pltpu.VMEM((ROWS, COLS, CHUNK, CH), BF16),
             pltpu.VMEM((pixels, CH), F32),
             pltpu.VMEM((2, WIDE, CH), F32),
-            dma((3,)), dma((5,)), dma((9,)), dma((5,)), dma((9,)), dma((FAR,)), dma((len(ESUBS),)),
+            dma((3,)), dma((5,)), dma((9,)), dma((5,)), dma((XBASE[-1],)), dma((FAR,)), dma((len(ESUBS),)),
         ],
         compiler_params=pltpu.CompilerParams(
             collective_id=0, has_side_effects=True, vmem_limit_bytes=48 * 1024 * 1024

time: 95.8 us -> 94.8 us (0.990)
  no operation moved by 1% of the time
where the time goes in v5:
time: 94.8 us; the launch traced here: 94.7 us
  Pallas kernels  93.9 us (99%)
    pallas_call x1, Pallas kernels, per_device(): pl.pallas_call(kernel, out_shape=jax.ShapeDtypeStruct((pixels, CH), BF16)...  93.9 us

profile of v5, /device:TPU:6, one launch (start us, length us, event | category | flops | bytes accessed | tf_op | source)
XLA Modules:
  0.0 94.7 jit_solution(5940083693981380796)
XLA Ops:
  0.0 93.9 %shard_map.82 = bf16[2304,128]{1,0:T(8,128)(2,1)S(1)} custom-call(bf16[2304,128]{1,0:T(8,128)(2,1)} %bitcast.4, bf16[128,128]{1,0:T(8,128)(2,1)} %lw_hbm.1, bf16[128,128]{1,0:T(8,128)(2,1)} %lg_hbm.1, bf16[128,128]{1,0:T(8,128)(2,1)} %rw_hbm.1, bf16[128,128]{1,0:T(8,128)(2,1)} %rg_hbm.1, f32[1,128]{1,0:T(1,128)} %bitcast.5, bf16[128,128]{1,0:T(8,128)(2,1)} %ow_hbm.1, ...), custom_call_target="tpu_custom_call" | custom-call | tf_op jit(solution)/shard_map/pallas_call | solution.py:440
  93.9 0.8 copy.10

commit v6 on v5

--- a/solution.py
+++ b/solution.py
@@ -14,9 +14,9 @@
 TEAM = 6
 FAR = (COLS - TEAM) // 2
 CHUNK = 2 * WIDE
-YSUBS = (((0, 2), (2, 6), (6, 10), (10, 16)), ((10, 16), (8, 10), (0, 2), (2, 4), (4, 8)))
-ESUBS = ((10, 16), (8, 10), (0, 2), (2, 4), (4, 6), (6, 8))
-HALVES = ((0, 1, 5, 4), (3, 2))
+YSUBS = (((0, 2), (2, 6), (6, 10), (10, 16)), ((10, 16), (0, 2), (2, 4), (4, 6), (6, 10)))
+ESUBS = ((10, 16), (0, 2), (2, 4), (4, 6), (6, 8), (8, 10))
+HALVES = ((0, 5, 4, 3), (2, 1))
 DIRECT = ((5,), (4, 3), (2, 1))
 ORDERS = [[0, 5, 4, 3, 2, 1]]
 while len(ORDERS) < TEAM - 1:
@@ -110,7 +110,7 @@
     loads[7].wait()
     xf[pl.ds(0, LINES * WIDE), :] = x_ref[...].astype(F32)
 
-    @pl.loop(0, WIDE // 2, unroll=3)
+    @pl.loop(0, WIDE // 2, unroll=6)
     def _(n):
         parts = []
         for i in (2 * n, 2 * n + 1):
@@ -125,7 +125,7 @@
             fac0[pl.ds(2 * n + m, 16, stride=WIDE), :] = value[:, CH * m : CH * m + CH]
 
     def project(arr):
-        @pl.loop(0, WIDE // 2, unroll=3)
+        @pl.loop(0, WIDE // 2, unroll=6)
         def _(n):
             xi = xr[pl.ds(pl.multiple_of(2 * CH * n, 2 * CH), 2 * CH), :]
             both = nt(wt[pl.ds(2 * CH * arr, 2 * CH), :], xi)
@@ -157,7 +157,7 @@
             first = pl.multiple_of((32 * y + 2 * team) * WIDE, 16)
             yb[arr, y, t] = facs[arr][pl.ds(first, CHUNK), :].astype(BF16)
 
-        for o in range(1, ROWS):
+        for o in (2, 1, 3):
             y_copy(arr, sub, o).start()
 
     def z_copy(arr, s, way):
@@ -235,7 +235,7 @@
             [fac0[pl.ds(first, WIDE), :] for first in rows], axis=0
         ).astype(BF16)
     pl.semaphore_wait(barrier, ROWS - 1 + len(steps))
-    for o in range(1, ROWS):
+    for o in (2, 1, 3):
         y_copy(0, 0, o).start()
 
     project(0)
@@ -373,7 +373,7 @@
                 es[q, t] = quarter(q)
             ds[y, t] = quarter(y)
 
-        for o in range(1, ROWS):
+        for o in (2, 1, 3):
             e_copy(sub, o).start()
 
     mixed = facl
@@ -405,7 +405,7 @@
 
     out = facr
 
-    @pl.loop(0, WIDE // 4)
+    @pl.loop(0, WIDE // 4, unroll=2)
     def _(n):
         scaled = []
         for j in range(4):

time: 94.8 us -> 94 us (level)
  Pallas kernels: 93.9 us -> 92.8 us
    pallas_call x1, Pallas kernels: 93.9 us -> 92.8 us  [per_device(): pl.pallas_call(kernel, out_shape=jax.ShapeDtypeStruct((pixels, CH), BF16)...]
where the time goes in v6:
time: 94 us; the launch traced here: 93.7 us
  Pallas kernels  92.8 us (99%)
    pallas_call x1, Pallas kernels, per_device(): pl.pallas_call(kernel, out_shape=jax.ShapeDtypeStruct((pixels, CH), BF16)...  92.8 us

profile of v6, /device:TPU:6, one launch (start us, length us, event | category | flops | bytes accessed | tf_op | source)
XLA Modules:
  0.0 93.7 jit_solution(5838385771758918912)
XLA Ops:
  0.0 92.8 %shard_map.82 = bf16[2304,128]{1,0:T(8,128)(2,1)S(1)} custom-call(bf16[2304,128]{1,0:T(8,128)(2,1)} %bitcast.4, bf16[128,128]{1,0:T(8,128)(2,1)} %lw_hbm.1, bf16[128,128]{1,0:T(8,128)(2,1)} %lg_hbm.1, bf16[128,128]{1,0:T(8,128)(2,1)} %rw_hbm.1, bf16[128,128]{1,0:T(8,128)(2,1)} %rg_hbm.1, f32[1,128]{1,0:T(1,128)} %bitcast.5, bf16[128,128]{1,0:T(8,128)(2,1)} %ow_hbm.1, ...), custom_call_target="tpu_custom_call" | custom-call | tf_op jit(solution)/shard_map/pallas_call | solution.py:440
  92.8 0.8 copy.10

commit v7 on v6

--- a/solution.py
+++ b/solution.py
@@ -390,7 +390,7 @@
                 total = total + block[:WIDE] + block[WIDE:]
             return total
 
-        total = lax.fori_loop(t0, t1, add, total)
+        total = lax.fori_loop(t0, t1, add, total, unroll=2)
     mean = total * (1.0 / CH)
 
     def spread(n, total):
@@ -399,13 +399,13 @@
             total = total + off * off
         return total
 
-    var = lax.fori_loop(0, CH // 8, spread, jnp.zeros((WIDE, CH), F32)) * (1.0 / CH)
+    var = lax.fori_loop(0, CH // 8, spread, jnp.zeros((WIDE, CH), F32), unroll=2) * (1.0 / CH)
     stat[0] = mean
     stat[1] = lax.rsqrt(var + 1e-05)
 
     out = facr
 
-    @pl.loop(0, WIDE // 4, unroll=2)
+    @pl.loop(0, WIDE // 4, unroll=6)
     def _(n):
         scaled = []
         for j in range(4):
@@ -420,7 +420,7 @@
                     CH * j + 32 * b : CH * j + 32 * b + 32
                 ]
 
-    @pl.loop(0, 6)
+    @pl.loop(0, 6, unroll=2)
     def _(n):
         rows = pl.ds(pl.multiple_of(n * 384, 384), 384)
         o_ref[rows, :] = (out[rows, :] * gt[rows, :]).astype(BF16)

time: 94 us -> 93.4 us (level)
  no operation moved by 1% of the time
where the time goes in v7:
time: 93.4 us; the launch traced here: 93.1 us
  Pallas kernels  92.3 us (99%)
    pallas_call x1, Pallas kernels, per_device(): pl.pallas_call(kernel, out_shape=jax.ShapeDtypeStruct((pixels, CH), BF16)...  92.3 us

profile of v7, /device:TPU:6, one launch (start us, length us, event | category | flops | bytes accessed | tf_op | source)
XLA Modules:
  0.0 93.1 jit_solution(3702542708263060682)
XLA Ops:
  0.0 92.3 %shard_map.82 = bf16[2304,128]{1,0:T(8,128)(2,1)S(1)} custom-call(bf16[2304,128]{1,0:T(8,128)(2,1)} %bitcast.4, bf16[128,128]{1,0:T(8,128)(2,1)} %lw_hbm.1, bf16[128,128]{1,0:T(8,128)(2,1)} %lg_hbm.1, bf16[128,128]{1,0:T(8,128)(2,1)} %rw_hbm.1, bf16[128,128]{1,0:T(8,128)(2,1)} %rg_hbm.1, f32[1,128]{1,0:T(1,128)} %bitcast.5, bf16[128,128]{1,0:T(8,128)(2,1)} %ow_hbm.1, ...), custom_call_target="tpu_custom_call" | custom-call | tf_op jit(solution)/shard_map/pallas_call | solution.py:440
  92.3 0.8 copy.10
